TPU v7x, 256 devices: a 8x8x2 block of a 8x8x16 slice. The times are simulated.
256 devices in a mesh: grp: 2 (over z), cand: 128 (over x, y, core).
Axes of the slice: x: 8, y: 8, z: 2, core: 2. Of those that a mesh axis runs over, the one named last changes fastest.
The devices are a block of a 8x8x16 slice.
Arguments:
- prompt_key_rows: bfloat16 [2048, 512], P(('grp', 'cand')), parts along dimension 0, may hold values from -6 to 6
- prompt_value_rows: bfloat16 [2048, 512], P(('grp', 'cand')), parts along dimension 0, may hold values from -6 to 6
- queries: bfloat16 [32768, 4096], P(('grp', 'cand')), parts along dimension 0, may hold values from -6 to 6
- keys: bfloat16 [32768, 512], P(('grp', 'cand')), parts along dimension 0, may hold values from -6 to 6
- values: bfloat16 [32768, 512], P(('grp', 'cand')), parts along dimension 0, may hold values from -6 to 6
- output_gradient: bfloat16 [32768, 4096], P(('grp', 'cand')), parts along dimension 0, may hold values from -12 to 12
- lengths: int32 [256], P(('grp', 'cand')), parts along dimension 0, may hold values from 1 to 120, 5120 in all
- prompt_visible_rows: int32 [256], P(('grp', 'cand')), parts along dimension 0, may hold values from 256 to 1024
- query_gain: float32 [128], replicated, may hold values from 0.25 to 1.75
- key_norm_gain: float32 [128], replicated, may hold values from 0.25 to 1.75
- key_value_weight: bfloat16 [5120, 1024], P('cand'), may hold values from -0.25 to 0.25
Outputs:
- query_grad: bfloat16 [32768, 4096], P(('grp', 'cand')), parts along dimension 0
- key_grad: bfloat16 [32768, 512], P(('grp', 'cand')), parts along dimension 0
- value_grad: bfloat16 [32768, 512], P(('grp', 'cand')), parts along dimension 0
- prompt_hidden_grad: bfloat16 [2048, 5120], P(('grp', 'cand')), parts along dimension 0
There are 2 independent parts, one for each index of `grp`. A program takes and returns all parts, laid end to end along the dimension named above; an argument that names none is the same for every part. Nothing has to cross between parts.
Inputs may be any that keep to these rules, and one draw needn't show every extreme that they name: The first lengths[c] of candidate c's 128 slots hold its response, the rest are padding.
All inputs are finite; a program needn't handle non-finite values. No bound on the sum of `lengths` on one device may be relied on, other than what follows from the above.
Results may differ from a plain program's by a relative error of at most 0.0098.
Values may be sent and summed in bfloat16 or wider, within the bound.
No kernel may reach another device: no remote copies, remote signals or barrier semaphores. Data moves between devices by JAX's collectives and lax.ppermute only.
A program may use at most 128 MiB of HBM per device.

v0:
```python
import functools

import jax
import jax.numpy as jnp
from jax import lax
from jax.experimental import pallas as pl
from jax.experimental.pallas import tpu as pltpu
from jax.sharding import Mesh
from jax.sharding import PartitionSpec as P

CAND = ("cand_0", "cand_1", "cand_2")
GRP_CAND = ("grp", "cand_0", "cand_1", "cand_2")
PLANE = ("cand_0", "cand_1")
FAR, NEAR, PAIR = CAND
ROW_SLOTS = 32
KEY_CHUNK = 128
LOG2_E = 1.4426950408889634

epsilon = 1e-06


def swap(x):
    return lax.ppermute(x, PAIR, [(0, 1), (1, 0)])


def from_everyone(shard, axis):
    copies = jnp.broadcast_to(shard, (lax.axis_size(axis), *shard.shape))
    return lax.all_to_all(copies, axis, split_axis=0, concat_axis=0, tiled=True)


def contract_last(left, right):
    return lax.dot_general(
        left, right, (((1,), (1,)), ((), ())), preferred_element_type=jnp.float32
    )


def contract_first(left, right):
    return lax.dot_general(
        left, right, (((0,), (0,)), ((), ())), preferred_element_type=jnp.float32
    )


def head_kernel(
    meta,
    q_own, g_own, k_own, v_own,
    q_other, g_other, k_other, v_other,
    prompt,
    q_gain, k_gain,
    dq_own, dk_own, dv_own, dq_other, dk_other, dv_other, prompt_grads,
    kn, vv, x_s, r_s, qs, gs, e_s, dp_s, ds_s, dk_acc, dv_acc,
):
    slots, width = q_own.shape
    head_dim = k_own.shape[1]
    group = width // head_dim
    prompt_total = prompt.shape[0]
    total = prompt_total + slots
    rows = ROW_SLOTS * group
    scale = head_dim ** (-0.5)
    gain_q, gain_k = q_gain[...], k_gain[...]

    kn[:prompt_total] = prompt[:, :head_dim]
    vv[:prompt_total] = prompt[:, head_dim:]
    dk_acc[:prompt_total] = jnp.zeros((prompt_total, head_dim), jnp.float32)
    dv_acc[:prompt_total] = jnp.zeros((prompt_total, head_dim), jnp.float32)

    units = (
        (0, q_own, g_own, k_own, v_own, dq_own, dk_own, dv_own),
        (1, q_other, g_other, k_other, v_other, dq_other, dk_other, dv_other),
    )
    for which, q_ref, g_ref, k_ref, v_ref, dq_ref, dk_ref, dv_ref in units:
        length, seen = meta[2 * which], meta[2 * which + 1]
        key_x = k_ref[...].astype(jnp.float32)
        key_r = lax.rsqrt(jnp.mean(key_x * key_x, axis=-1, keepdims=True) + epsilon)
        kn[prompt_total:] = (key_x * key_r * gain_k).astype(jnp.bfloat16)
        vv[prompt_total:] = v_ref[...]
        dk_acc[prompt_total:] = jnp.zeros((slots, head_dim), jnp.float32)
        dv_acc[prompt_total:] = jnp.zeros((slots, head_dim), jnp.float32)
        dq_ref[...] = jnp.zeros(dq_ref.shape, dq_ref.dtype)

        def row_block(b, carry, length=length, seen=seen, q_ref=q_ref, g_ref=g_ref, dq_ref=dq_ref):
            first = pl.multiple_of(b * ROW_SLOTS, ROW_SLOTS)
            at = pl.ds(first, ROW_SLOTS)
            live = (
                lax.broadcasted_iota(jnp.int32, (ROW_SLOTS, head_dim), 0) + first < length
            )
            for g in range(group):
                cols = slice(g * head_dim, (g + 1) * head_dim)
                mine = slice(g * ROW_SLOTS, (g + 1) * ROW_SLOTS)
                x = q_ref[at, cols].astype(jnp.float32)
                r = lax.rsqrt(jnp.mean(x * x, axis=-1, keepdims=True) + epsilon)
                x_s[mine] = x
                r_s[mine] = jnp.broadcast_to(r, x.shape)
                qs[mine] = (x * r * gain_q).astype(jnp.bfloat16)
                grad = g_ref[at, cols].astype(jnp.float32)
                gs[mine] = jnp.where(live, grad, 0.0).astype(jnp.bfloat16)
            q, go = qs[...], gs[...]
            sums = jnp.zeros((8, rows), jnp.float32)
            dots = jnp.zeros((8, rows), jnp.float32)
            for base in range(0, total, KEY_CHUNK):
                chunk = slice(base, base + KEY_CHUNK)
                index = lax.broadcasted_iota(jnp.int32, (KEY_CHUNK, rows), 0)
                if base < prompt_total:
                    visible = index < seen - base
                else:
                    slot = lax.broadcasted_iota(jnp.int32, (KEY_CHUNK, rows), 1)
                    slot = (slot & (ROW_SLOTS - 1)) + first
                    visible = index + (base - prompt_total) <= slot
                s = contract_last(kn[chunk], q)
                e = jnp.where(visible, jnp.exp2(s * (scale * LOG2_E)), 0.0)
                dp = contract_last(vv[chunk], go)
                e_s[chunk] = e
                dp_s[chunk] = dp
                sums += jnp.sum(e.reshape(KEY_CHUNK // 8, 8, rows), axis=0)
                dots += jnp.sum((e * dp).reshape(KEY_CHUNK // 8, 8, rows), axis=0)
            inverse = 1.0 / jnp.sum(sums, axis=0, keepdims=True)
            delta = jnp.sum(dots, axis=0, keepdims=True) * inverse
            for base in range(0, total, KEY_CHUNK):
                chunk = slice(base, base + KEY_CHUNK)
                p = e_s[chunk] * inverse
                ds = (p * (dp_s[chunk] - delta)).astype(jnp.bfloat16)
                ds_s[chunk] = ds
                dv_acc[chunk] += jnp.dot(
                    p.astype(jnp.bfloat16), go, preferred_element_type=jnp.float32
                )
                dk_acc[chunk] += jnp.dot(ds, q, preferred_element_type=jnp.float32)
            dq = contract_first(ds_s[...], kn[...]) * scale
            x, r = x_s[...], r_s[...]
            w = dq * gain_q
            inner = jnp.mean(w * x, axis=-1, keepdims=True)
            dx = (r * w - x * (r * r * r) * inner).astype(jnp.bfloat16)
            for g in range(group):
                dq_ref[at, g * head_dim : (g + 1) * head_dim] = dx[
                    g * ROW_SLOTS : (g + 1) * ROW_SLOTS
                ]
            return carry

        lax.fori_loop(0, (length + (ROW_SLOTS - 1)) // ROW_SLOTS, row_block, 0)
        w = dk_acc[prompt_total:] * scale * gain_k
        inner = jnp.mean(w * key_x, axis=-1, keepdims=True)
        dk_ref[...] = (key_r * w - key_x * (key_r * key_r * key_r) * inner).astype(jnp.bfloat16)
        dv_ref[...] = dv_acc[prompt_total:].astype(jnp.bfloat16)
    prompt_grads[:, :head_dim] = (dk_acc[:prompt_total] * scale).astype(jnp.bfloat16)
    prompt_grads[:, head_dim:] = dv_acc[:prompt_total].astype(jnp.bfloat16)


def attend(heads, meta, own, other, prompt, q_gain, k_gain, width, head_dim):
    slots, total = own.shape[0], prompt.shape[0]
    keys = total + slots
    group = width // head_dim
    rows = ROW_SLOTS * group
    narrow = 2 * heads * group

    def columns(block, index):
        return pl.BlockSpec((slots, block), lambda i, index=index: (0, index + i))

    def by_head(rows, block):
        return pl.BlockSpec((rows, block), lambda i: (0, i))

    def whole(shape):
        return pl.BlockSpec(shape, lambda i: (0, 0))

    side = [
        columns(width, 0),
        columns(width, heads),
        columns(head_dim, narrow),
        columns(head_dim, narrow + heads),
    ]
    low = jnp.bfloat16
    outs = [(slots, width), (slots, head_dim), (slots, head_dim)] * 2 + [(total, 2 * head_dim)]
    work = heads * 2 * 5 * 2 * slots * group * keys * head_dim
    return pl.pallas_call(
        head_kernel,
        grid=(heads,),
        in_specs=[pl.BlockSpec(memory_space=pltpu.SMEM)]
        + side
        + side
        + [by_head(total, 2 * head_dim), whole((1, head_dim)), whole((1, head_dim))],
        out_specs=[by_head(*s) for s in outs],
        out_shape=[jax.ShapeDtypeStruct((n, heads * m), low) for n, m in outs],
        scratch_shapes=[
            pltpu.VMEM((keys, head_dim), low),
            pltpu.VMEM((keys, head_dim), low),
            pltpu.VMEM((rows, head_dim), jnp.float32),
            pltpu.VMEM((rows, head_dim), jnp.float32),
            pltpu.VMEM((rows, head_dim), low),
            pltpu.VMEM((rows, head_dim), low),
            pltpu.VMEM((keys, rows), jnp.float32),
            pltpu.VMEM((keys, rows), jnp.float32),
            pltpu.VMEM((keys, rows), low),
            pltpu.VMEM((keys, head_dim), jnp.float32),
            pltpu.VMEM((keys, head_dim), jnp.float32),
        ],
        compiler_params=pltpu.CompilerParams(vmem_limit_bytes=24 * 1024 * 1024),
        cost_estimate=pl.CostEstimate(
            flops=work, bytes_accessed=heads * 4 * 1024 * 1024,
            transcendentals=heads * 2 * slots * group * keys,
        ),
    )(meta, own, own, own, own, other, other, other, other, prompt, q_gain, k_gain)


def on_device(
    prompt_key_rows,
    prompt_value_rows,
    queries,
    keys,
    values,
    output_gradient,
    lengths,
    prompt_visible_rows,
    query_gain,
    key_norm_gain,
    key_value_weight,
):
    head_dim = query_gain.shape[0]
    core = lax.axis_index(PAIR)
    cores = lax.axis_size(PAIR)
    heads = keys.shape[1] // head_dim // cores
    narrow = heads * head_dim
    wide = queries.shape[1] // cores
    width = wide // heads
    near, far = lax.axis_size(NEAR), lax.axis_size(FAR)
    q_gain, k_gain = query_gain[None, :], key_norm_gain[None, :]

    def part(a, which, n):
        return lax.dynamic_slice_in_dim(a, which * n, n, axis=1)

    def in_core_order(mine, theirs):
        flip = core == 0
        return jnp.where(flip, mine, theirs), jnp.where(flip, theirs, mine)

    def prompt_part(which):
        return jnp.concatenate(
            [part(prompt_key_rows, which, narrow), part(prompt_value_rows, which, narrow)], axis=1
        )

    def pack(which):
        return jnp.concatenate(
            [
                part(queries, which, wide),
                part(output_gradient, which, wide),
                part(keys, which, narrow),
                part(values, which, narrow),
            ],
            axis=1,
        )

    def weight_part(which):
        cut = key_value_weight.reshape(-1, 2, cores, heads, head_dim)
        cut = lax.dynamic_index_in_dim(cut, which, 2, keepdims=False)
        return cut.transpose(0, 2, 1, 3).reshape(-1, 2 * narrow)

    raw = jnp.concatenate(in_core_order(prompt_part(core), swap(prompt_part(1 - core))), axis=0)
    count = raw.shape[0]
    px = raw[:, :narrow].astype(jnp.float32).reshape(count, heads, head_dim)
    pr = lax.rsqrt(jnp.mean(px * px, axis=-1, keepdims=True) + epsilon)
    pn = (px * pr * key_norm_gain).astype(jnp.bfloat16).reshape(count, narrow)
    pv = raw[:, narrow:]

    meta_own = jnp.stack([lengths[0], prompt_visible_rows[0]])
    meta = jnp.concatenate([meta_own, swap(meta_own)])
    own, other = pack(core), swap(pack(1 - core))
    weight_pair = jnp.concatenate(
        in_core_order(weight_part(core), swap(weight_part(1 - core))), axis=0
    )

    both = jnp.concatenate(
        [
            a[:, h * head_dim : (h + 1) * head_dim]
            for h in range(heads)
            for a in (pn, pv)
        ],
        axis=1,
    )
    prompt = from_everyone(both, PLANE).reshape(-1, 2 * narrow)
    weight = from_everyone(weight_pair, FAR).reshape(-1, 2 * narrow)

    results = attend(heads, meta, own, other, prompt, q_gain, k_gain, width, head_dim)

    sent = results[6].reshape(far * near, count, 2 * narrow)
    parts = lax.all_to_all(sent, PLANE, 0, 0, tiled=True)
    total = jnp.sum(parts.astype(jnp.float32), axis=0).reshape(count, heads, 2, head_dim)
    w = total[:, :, 0] * key_norm_gain
    inner = jnp.mean(w * px, axis=-1, keepdims=True)
    dk = pr * w - px * (pr * pr * pr) * inner
    grads = jnp.stack([dk, total[:, :, 1]], axis=2).reshape(count, 2 * narrow)
    rows = from_everyone(grads.astype(jnp.bfloat16), NEAR).reshape(-1, 2 * narrow)

    def assembled(index):
        return jnp.concatenate(in_core_order(results[index], swap(results[index + 3])), axis=1)

    query_grad, key_grad, value_grad = assembled(0), assembled(1), assembled(2)

    hidden = contract_last(rows, weight)
    per_core = count // cores
    hidden = hidden.reshape(near, cores, per_core, -1)
    mine = lax.dynamic_index_in_dim(hidden, core, 1, keepdims=False)
    theirs = lax.dynamic_index_in_dim(hidden, 1 - core, 1, keepdims=False)
    mine = (mine + swap(theirs.astype(jnp.bfloat16)).astype(jnp.float32)).astype(jnp.bfloat16)
    arrived = lax.all_to_all(mine, NEAR, 0, 0, tiled=True)
    arrived = arrived.reshape(near, per_core, far, -1)
    hidden_grad = arrived.transpose(1, 2, 0, 3).reshape(per_core, -1)
    return (query_grad, key_grad, value_grad, hidden_grad)


def solution(mesh):
    finer = Mesh(
        mesh.devices.reshape(mesh.shape["grp"], 8, 8, 2), ("grp", "cand_0", "cand_1", "cand_2")
    )
    return jax.shard_map(
        on_device,
        mesh=finer,
        in_specs=(
            P(GRP_CAND, None),
            P(GRP_CAND, None),
            P(GRP_CAND, None),
            P(GRP_CAND, None),
            P(GRP_CAND, None),
            P(GRP_CAND, None),
            P(GRP_CAND),
            P(GRP_CAND),
            P(),
            P(),
            P(CAND, None),
        ),
        out_specs=(P(GRP_CAND, None), P(GRP_CAND, None), P(GRP_CAND, None), P(GRP_CAND, None)),
        check_vma=False,
    )
```

profile of v0, /device:TPU:513, one launch (start us, length us, event | category | flops | bytes accessed | tf_op | source)
XLA Modules:
  0.0 174.4 jit_solution(5497252408856023401)
XLA Ops:
  0.6 0.7 constant_dynamic-slice_fusion.4
  1.4 20.4 %collective-permute-start.2 = (bf16[8,512]{1,0:T(8,128)(2,1)S(1)}, bf16[8,512]{1,0:T(8,128)(2,1)S(1)}, u32[]{:S(2)}, u32[]{:S(2)}) collective-permute-start(bf16[8,512]{1,0:T(8,128)(2,1)S(1)} %pad_maximum_fusion.8), channel_id=1, source_target_pairs={{0,1},{1,0},{2,3},{3,2},{4,5},{5,4},{6,7},{7,6},{8,9},{9,8},{10,11... | collective-permute-start | bytes 24584 | tf_op jit(solution)/shard_map/ppermute | solution.py:23
  21.8 0.7 broadcast_bitcast_fusion
  22.5 0.2 collective-permute-done.2
  22.6 0.0 copy-start.8
  22.7 0.0 copy-start.10
  22.7 0.1 multiply_reduce_fusion.1
  22.8 0.6 multiply_multiply_fusion
  23.4 0.1 mul.123
  23.5 0.5 copy-done.13
  24.0 0.0 copy-start.11
  24.0 1.1 broadcast_in_dim.19
  25.1 6.6 %all-to-all-start = ((bf16[64,16,512]{2,1,0:T(8,128)(2,1)}), bf16[64,16,512]{2,1,0:T(8,128)(2,1)S(1)}, u32[]{:S(2)}, u32[]{:S(2)}) async-start(bf16[64,16,512]{2,1,0:T(8,128)(2,1)} %broadcast_in_dim.19), calls=%async_computation | async-start | bytes 2097152 | tf_op jit(solution)/shard_map/all_to_all | solution.py:28
  31.8 0.9 constant_dynamic-slice_fusion.6
  32.7 0.2 constant_dynamic-slice_fusion.8
  32.9 0.1 pad_maximum_fusion.1
  33.0 0.5 collective-permute-start.1
  34.7 0.1 pad_add_fusion
  34.8 0.2 collective-permute-start
  35.0 0.1 pad_maximum_fusion.q_own.g_own.k_own.v_own
  35.1 0.9 collective-permute-done
  36.0 0.1 pad_add_fusion.1.meta
  36.1 0.0 collective-permute-done.1.q_other.g_other.k_other.v_other
  36.1 1.0 copy-done.1
  37.2 21.1 %all-to-all-done = bf16[64,16,512]{2,1,0:T(8,128)(2,1)S(1)} async-done(((bf16[64,16,512]{2,1,0:T(8,128)(2,1)}), bf16[64,16,512]{2,1,0:T(8,128)(2,1)S(1)}, u32[]{:S(2)}, u32[]{:S(2)}) %all-to-all-start) | async-done | bytes 1048608 | tf_op jit(solution)/shard_map/all_to_all | solution.py:28
  58.3 1.3 copy-done.2
  59.5 8.3 %shard_map.138 = (bf16[128,2048]{1,0:T(8,128)(2,1)S(1)}, bf16[128,256]{1,0:T(8,128)(2,1)S(1)}, bf16[128,256]{1,0:T(8,128)(2,1)S(1)}, bf16[128,2048]{1,0:T(8,128)...) custom-call(s32[4]{0:T(128)S(1)} %pad_add_fusion.1.meta, ...), custom_call_target="tpu_custom_call" | custom-call | flops 6039797760 | bytes 8388608 | tf_op jit(solution)/shard_map/pallas_call | solution.py:171
  67.9 26.1 %all-to-all-start.1 = ((bf16[64,16,512]{2,1,0:T(8,128)(2,1)}), bf16[64,16,512]{2,1,0:T(8,128)(2,1)S(1)}, u32[]{:S(2)}, u32[]{:S(2)}) async-start(bf16[64,16,512]{2,1,0:T(8,128)(2,1)} %bitcast.4), calls=%async_computation.1 | async-start | bytes 2097152 | tf_op jit(solution)/shard_map/all_to_all | solution.py:280
  94.0 0.1 constant_dynamic-slice_fusion.1
  94.2 1.8 %collective-permute-start.6 = (bf16[40,512]{1,0:T(8,128)(2,1)S(1)}, bf16[40,512]{1,0:T(8,128)(2,1)S(1)}, u32[]{:S(2)}, u32[]{:S(2)}) collective-permute-start(bf16[40,512]{1,0:T(8,128)(2,1)S(1)} %reshape.90), channel_id=1, source_target_pairs={{0,1},{1,0},{2,3},{3,2},{4,5},{5,4},{6,7},{7,6},{8,9},{9,8},{10,11... | collective-permute-start | bytes 122888 | tf_op jit(solution)/shard_map/ppermute | solution.py:23
  96.1 0.6 reshape.87
  96.7 0.2 collective-permute-done.6
  96.9 0.5 collective-permute-start.5
  97.4 0.2 collective-permute-start.4
  97.6 0.3 collective-permute-start.3
  97.9 21.6 %all-to-all-done.1 = bf16[64,16,512]{2,1,0:T(8,128)(2,1)S(1)} async-done(((bf16[64,16,512]{2,1,0:T(8,128)(2,1)}), bf16[64,16,512]{2,1,0:T(8,128)(2,1)S(1)}, u32[]{:S(2)}, u32[]{:S(2)}) %all-to-all-start.1) | async-done | bytes 1048608 | tf_op jit(solution)/shard_map/all_to_all | solution.py:280
  119.5 0.9 broadcast_in_dim.23
  120.4 5.8 %all-to-all-start.3 = ((bf16[8,80,512]{2,1,0:T(8,128)(2,1)}), bf16[8,80,512]{2,1,0:T(8,128)(2,1)S(1)}, u32[]{:S(2)}, u32[]{:S(2)}) async-start(bf16[8,80,512]{2,1,0:T(8,128)(2,1)} %broadcast_in_dim.23), calls=%async_computation.3 | async-start | bytes 1310720 | tf_op jit(solution)/shard_map/all_to_all | solution.py:28
  126.2 0.0 collective-permute-done.5
  126.2 1.5 broadcast_select_fusion.3
  127.7 0.0 collective-permute-done.4
  127.7 1.5 broadcast_select_fusion.5
  129.2 0.8 convert_reduce_fusion
  130.0 0.8 reshape.86
  130.9 0.8 multiply_reduce_fusion
  131.7 0.9 subtract_convert_fusion
  132.7 11.4 %all-to-all-done.3 = bf16[8,80,512]{2,1,0:T(8,128)(2,1)S(1)} async-done(((bf16[8,80,512]{2,1,0:T(8,128)(2,1)}), bf16[8,80,512]{2,1,0:T(8,128)(2,1)S(1)}, u32[]{:S(2)}, u32[]{:S(2)}) %all-to-all-start.3) | async-done | bytes 655392 | tf_op jit(solution)/shard_map/all_to_all | solution.py:28
  144.1 0.7 broadcast_in_dim.22
  144.7 4.7 %all-to-all-start.2 = ((bf16[8,16,512]{2,1,0:T(8,128)(2,1)}), bf16[8,16,512]{2,1,0:T(8,128)(2,1)S(1)}, u32[]{:S(2)}, u32[]{:S(2)}) async-start(bf16[8,16,512]{2,1,0:T(8,128)(2,1)} %broadcast_in_dim.22), calls=%async_computation.2 | async-start | bytes 262144 | tf_op jit(solution)/shard_map/all_to_all | solution.py:28
  149.4 0.7 pad_maximum_fusion.4
  150.1 0.7 pad_maximum_fusion.3
  150.7 6.7 %all-to-all-done.2 = bf16[8,16,512]{2,1,0:T(8,128)(2,1)S(1)} async-done(((bf16[8,16,512]{2,1,0:T(8,128)(2,1)}), bf16[8,16,512]{2,1,0:T(8,128)(2,1)S(1)}, u32[]{:S(2)}, u32[]{:S(2)}) %all-to-all-start.2) | async-done | bytes 131104 | tf_op jit(solution)/shard_map/all_to_all | solution.py:28
  157.4 0.4 fusion.1
  157.8 3.3 %collective-permute-start.7 = (bf16[8,8,640]{2,1,0:T(8,128)(2,1)S(1)}, bf16[8,8,640]{2,1,0:T(8,128)(2,1)S(1)}, u32[]{:S(2)}, u32[]{:S(2)}) collective-permute-start(bf16[8,8,640]{2,1,0:T(8,128)(2,1)S(1)} %fusion.3), channel_id=1, source_target_pairs={{0,1},{1,0},{2,3},{3,2},{4,5},{5,4},{6,7},{7,6},{8,9},{9,8},{10,11... | collective-permute-start | bytes 245768 | tf_op jit(solution)/shard_map/ppermute | solution.py:23
  161.1 0.0 collective-permute-done.3
  161.1 0.1 broadcast_select_fusion.1
  161.2 0.8 collective-permute-done.7
  162.0 0.7 fusion
  162.7 3.6 %all-to-all-start.4 = ((bf16[8,8,640]{2,1,0:T(8,128)(2,1)}), bf16[8,8,640]{2,1,0:T(8,128)(2,1)S(1)}, u32[]{:S(2)}, u32[]{:S(2)}) async-start(bf16[8,8,640]{2,1,0:T(8,128)(2,1)} %fusion), calls=%async_computation.4 | async-start | bytes 163840 | tf_op jit(solution)/shard_map/all_to_all | solution.py:299
  166.3 1.0 pad_maximum_fusion.2
  167.3 6.0 %all-to-all-done.4 = bf16[8,8,640]{2,1,0:T(8,128)(2,1)S(1)} async-done(((bf16[8,8,640]{2,1,0:T(8,128)(2,1)}), bf16[8,8,640]{2,1,0:T(8,128)(2,1)S(1)}, u32[]{:S(2)}, u32[]{:S(2)}) %all-to-all-start.4) | async-done | bytes 81952 | tf_op jit(solution)/shard_map/all_to_all | solution.py:299
  173.3 0.2 reshape.92
  173.4 0.1 copy.21
  173.5 0.8 reshape.93
  (46 shorter events, 0.4 us)
Async XLA Ops:
  1.4 21.2 %collective-permute-start.2 = (bf16[8,512]{1,0:T(8,128)(2,1)S(1)}, bf16[8,512]{1,0:T(8,128)(2,1)S(1)}, u32[]{:S(2)}, u32[]{:S(2)}) collective-permute-start(bf16[8,512]{1,0:T(8,128)(2,1)S(1)} %pad_maximum_fusion.8), channel_id=1, source_target_pairs={{0,1},{1,0},{2,3},{3,2},{4,5},{5,4},{6,7},{7,6},{8,9},{9,8},{10,11... | collective-permute-start | bytes 24584 | tf_op jit(solution)/shard_map/ppermute | solution.py:23
  22.6 1.4 copy-start.8
  22.7 1.3 copy-start.10
  23.4 0.6 copy-start.13
  24.0 7.8 %copy-start.11 = (bf16[128,512]{1,0:T(8,128)(2,1)S(1)}, bf16[128,512]{1,0:T(8,128)(2,1)}, u32[]{:S(2)}) copy-start(bf16[128,512]{1,0:T(8,128)(2,1)} %param.15) | copy-start | bytes 393220
  25.1 7.6 %copy-start.4 = (bf16[128,4096]{1,0:T(8,128)(2,1)S(1)}, bf16[128,4096]{1,0:T(8,128)(2,1)}, u32[]{:S(2)}) copy-start(bf16[128,4096]{1,0:T(8,128)(2,1)} %param.16) | copy-start | bytes 3145732
  25.1 7.6 %copy-start.5 = (bf16[128,4096]{1,0:T(8,128)(2,1)S(1)}, bf16[128,4096]{1,0:T(8,128)(2,1)}, u32[]{:S(2)}) copy-start(bf16[128,4096]{1,0:T(8,128)(2,1)} %param.13) | copy-start | bytes 3145732
  25.1 33.2 %all-to-all-start = ((bf16[64,16,512]{2,1,0:T(8,128)(2,1)}), bf16[64,16,512]{2,1,0:T(8,128)(2,1)S(1)}, u32[]{:S(2)}, u32[]{:S(2)}) async-start(bf16[64,16,512]{2,1,0:T(8,128)(2,1)} %broadcast_in_dim.19), calls=%async_computation | async-start | bytes 2097152 | tf_op jit(solution)/shard_map/all_to_all | solution.py:28
  33.0 3.1 %collective-permute-start.1 = (bf16[128,4608]{1,0:T(8,128)(2,1)S(1)}, bf16[128,4608]{1,0:T(8,128)(2,1)S(1)}, u32[]{:S(2)}, u32[]{:S(2)}) collective-permute-start(bf16[128,4608]{1,0:T(8,128)(2,1)S(1)} %pad_maximum_fusion.1), channel_id=1, source_target_pairs={{0,1},{1,0},{2,3},{3,2},{4,5},{5,4},{6,7},{7,6},{8,9},{9,8},{10,11... | collective-permute-start | bytes 3538952 | tf_op jit(solution)/shard_map/ppermute | solution.py:23
  34.8 1.2 collective-permute-start
  35.0 23.2 %copy-start = (f32[128]{0:T(128)S(1)}, f32[128]{0:T(128)}, u32[]{:S(2)}) copy-start(f32[128]{0:T(128)} %param.20) | copy-start | bytes 1540
  35.0 23.2 %copy-start.3 = (f32[128]{0:T(128)S(1)}, f32[128]{0:T(128)}, u32[]{:S(2)}) copy-start(f32[128]{0:T(128)} %param.19) | copy-start | bytes 1540
  36.1 1.0 copy-start.1
  58.3 1.3 copy-start.2
  67.9 26.1 %copy-start.12 = (bf16[40,1024]{1,0:T(8,128)(2,1)S(1)}, bf16[40,1024]{1,0:T(8,128)(2,1)}, u32[]{:S(2)}) copy-start(bf16[40,1024]{1,0:T(8,128)(2,1)} %param.21) | copy-start | bytes 245764
  67.9 28.2 %copy-start.9 = (f32[16,256]{1,0:T(8,128)S(1)}, f32[16,256]{1,0:T(8,128)}, u32[]{:S(2)}) copy-start(f32[16,256]{1,0:T(8,128)} %copy-done.8) | copy-start | bytes 49156
  67.9 51.7 %all-to-all-start.1 = ((bf16[64,16,512]{2,1,0:T(8,128)(2,1)}), bf16[64,16,512]{2,1,0:T(8,128)(2,1)S(1)}, u32[]{:S(2)}, u32[]{:S(2)}) async-start(bf16[64,16,512]{2,1,0:T(8,128)(2,1)} %bitcast.4), calls=%async_computation.1 | async-start | bytes 2097152 | tf_op jit(solution)/shard_map/all_to_all | solution.py:280
  94.2 2.7 %collective-permute-start.6 = (bf16[40,512]{1,0:T(8,128)(2,1)S(1)}, bf16[40,512]{1,0:T(8,128)(2,1)S(1)}, u32[]{:S(2)}, u32[]{:S(2)}) collective-permute-start(bf16[40,512]{1,0:T(8,128)(2,1)S(1)} %reshape.90), channel_id=1, source_target_pairs={{0,1},{1,0},{2,3},{3,2},{4,5},{5,4},{6,7},{7,6},{8,9},{9,8},{10,11... | collective-permute-start | bytes 122888 | tf_op jit(solution)/shard_map/ppermute | solution.py:23
  96.9 29.3 %collective-permute-start.5 = (bf16[128,256]{1,0:T(8,128)(2,1)S(1)}, bf16[128,256]{1,0:T(8,128)(2,1)}, u32[]{:S(2)}, u32[]{:S(2)}) collective-permute-start(bf16[128,256]{1,0:T(8,128)(2,1)S(1)} %get-tuple-element.16), channel_id=1, source_target_pairs={{0,1},{1,0},{2,3},{3,2},{4,5},{5,4},{6,7},{7,6},{8,9},{9,8},{10,11... | collective-permute-start | bytes 196616 | tf_op jit(solution)/shard_map/ppermute | solution.py:23
  97.4 30.3 %collective-permute-start.4 = (bf16[128,256]{1,0:T(8,128)(2,1)S(1)}, bf16[128,256]{1,0:T(8,128)(2,1)}, u32[]{:S(2)}, u32[]{:S(2)}) collective-permute-start(bf16[128,256]{1,0:T(8,128)(2,1)S(1)} %get-tuple-element.14), channel_id=1, source_target_pairs={{0,1},{1,0},{2,3},{3,2},{4,5},{5,4},{6,7},{7,6},{8,9},{9,8},{10,11... | collective-permute-start | bytes 196616 | tf_op jit(solution)/shard_map/ppermute | solution.py:23
  97.6 63.5 %collective-permute-start.3 = (bf16[128,2048]{1,0:T(8,128)(2,1)S(1)}, bf16[128,2048]{1,0:T(8,128)(2,1)S(1)}, u32[]{:S(2)}, u32[]{:S(2)}) collective-permute-start(bf16[128,2048]{1,0:T(8,128)(2,1)S(1)} %get-tuple-element.12), channel_id=1, source_target_pairs={{0,1},{1,0},{2,3},{3,2},{4,5},{5,4},{6,7},{7,6},{8,9},{9,8},{10,11... | collective-permute-start | bytes 1572872 | tf_op jit(solution)/shard_map/ppermute | solution.py:23
  120.4 23.6 %all-to-all-start.3 = ((bf16[8,80,512]{2,1,0:T(8,128)(2,1)}), bf16[8,80,512]{2,1,0:T(8,128)(2,1)S(1)}, u32[]{:S(2)}, u32[]{:S(2)}) async-start(bf16[8,80,512]{2,1,0:T(8,128)(2,1)} %broadcast_in_dim.23), calls=%async_computation.3 | async-start | bytes 1310720 | tf_op jit(solution)/shard_map/all_to_all | solution.py:28
  126.2 5.5 %copy-start.14 = (f32[16,2]{1,0:T(8,128)S(1)}, f32[16,2]{1,0:T(8,128)}, u32[]{:S(2)}) copy-start(f32[16,2]{1,0:T(8,128)} %copy-done.13) | copy-start | bytes 388
  127.7 21.7 %copy-start.6 = (bf16[128,256]{1,0:T(8,128)(2,1)S(1)}, bf16[128,256]{1,0:T(8,128)(2,1)}, u32[]{:S(2)}) copy-start(bf16[128,256]{1,0:T(8,128)(2,1)} %get-tuple-element.25) | copy-start | bytes 196612
  129.2 20.8 %copy-start.7 = (bf16[128,256]{1,0:T(8,128)(2,1)S(1)}, bf16[128,256]{1,0:T(8,128)(2,1)}, u32[]{:S(2)}) copy-start(bf16[128,256]{1,0:T(8,128)(2,1)} %get-tuple-element.27) | copy-start | bytes 196612
  144.7 12.7 %all-to-all-start.2 = ((bf16[8,16,512]{2,1,0:T(8,128)(2,1)}), bf16[8,16,512]{2,1,0:T(8,128)(2,1)S(1)}, u32[]{:S(2)}, u32[]{:S(2)}) async-start(bf16[8,16,512]{2,1,0:T(8,128)(2,1)} %broadcast_in_dim.22), calls=%async_computation.2 | async-start | bytes 262144 | tf_op jit(solution)/shard_map/all_to_all | solution.py:28
  157.8 4.2 %collective-permute-start.7 = (bf16[8,8,640]{2,1,0:T(8,128)(2,1)S(1)}, bf16[8,8,640]{2,1,0:T(8,128)(2,1)S(1)}, u32[]{:S(2)}, u32[]{:S(2)}) collective-permute-start(bf16[8,8,640]{2,1,0:T(8,128)(2,1)S(1)} %fusion.3), channel_id=1, source_target_pairs={{0,1},{1,0},{2,3},{3,2},{4,5},{5,4},{6,7},{7,6},{8,9},{9,8},{10,11... | collective-permute-start | bytes 245768 | tf_op jit(solution)/shard_map/ppermute | solution.py:23
  162.7 10.6 %all-to-all-start.4 = ((bf16[8,8,640]{2,1,0:T(8,128)(2,1)}), bf16[8,8,640]{2,1,0:T(8,128)(2,1)S(1)}, u32[]{:S(2)}, u32[]{:S(2)}) async-start(bf16[8,8,640]{2,1,0:T(8,128)(2,1)} %fusion), calls=%async_computation.4 | async-start | bytes 163840 | tf_op jit(solution)/shard_map/all_to_all | solution.py:299
where the time goes:
time: 175 us; the launch traced here: 174 us
  starting transfers between devices  74 us (42%)
  waiting for transfers between devices  68.8 us (39%)
  local copies, waits for them, and re-layouts  10.9 us (6%)
  other arithmetic  9.74 us (6%)
  Pallas kernels  8.34 us (5%)
  between operations  2.26 us (1%)
    all_to_all x3, waiting for transfers between devices, from_everyone(): return lax.all_to_all(copies, axis, split_axis=0, concat_axis=0, tiled=True)  39.2 us
    ppermute x8, starting transfers between devices, swap(): return lax.ppermute(x, PAIR, [(0, 1), (1, 0)])  27.2 us
    all_to_all x1, starting transfers between devices, on_device(): parts = lax.all_to_all(sent, PLANE, 0, 0, tiled=True)  26.1 us
    all_to_all x1, waiting for transfers between devices, on_device(): parts = lax.all_to_all(sent, PLANE, 0, 0, tiled=True)  21.6 us
    all_to_all x3, starting transfers between devices, from_everyone(): return lax.all_to_all(copies, axis, split_axis=0, concat_axis=0, tiled=True)  17.1 us
    pallas_call x1, Pallas kernels, attend(): pl.pallas_call(head_kernel, grid=(heads,), in_specs=[pl.BlockSpec(memory_...  8.34 us
    all_to_all x1, waiting for transfers between devices, on_device(): arrived = lax.all_to_all(mine, NEAR, 0, 0, tiled=True)  5.98 us
    all_to_all x1, starting transfers between devices, on_device(): arrived = lax.all_to_all(mine, NEAR, 0, 0, tiled=True)  3.56 us
  transfers between devices with their start and end apart: 13, of which 9 were waited for; matrix products, arithmetic and copies ran while one was open for 8% of the time, Pallas kernels for 0%

commit v1 on v0

v1 whole, which is shorter than its diff:
```python
import functools

import jax
import jax.numpy as jnp
from jax import lax
from jax.experimental import pallas as pl
from jax.experimental.pallas import tpu as pltpu
from jax.sharding import Mesh
from jax.sharding import PartitionSpec as P

CAND = ("cand_0", "cand_1", "cand_2")
GRP_CAND = ("grp", "cand_0", "cand_1", "cand_2")
PLANE = ("cand_0", "cand_1")
FAR, NEAR, PAIR = CAND
ROW_SLOTS = 32
KEY_CHUNK = 128
KEY_STEPS = 4
LOG2_E = 1.4426950408889634

epsilon = 1e-06


def swap(x):
    return lax.ppermute(x, PAIR, [(0, 1), (1, 0)])


def from_everyone(shard, axis):
    copies = jnp.broadcast_to(shard, (lax.axis_size(axis), *shard.shape))
    return lax.all_to_all(copies, axis, split_axis=0, concat_axis=0, tiled=True)


def contract_last(left, right):
    return lax.dot_general(
        left, right, (((1,), (1,)), ((), ())), preferred_element_type=jnp.float32
    )


def contract_first(left, right):
    return lax.dot_general(
        left, right, (((0,), (0,)), ((), ())), preferred_element_type=jnp.float32
    )


def head_norm(x, gain):
    r = lax.rsqrt(jnp.mean(x * x, axis=-1, keepdims=True) + epsilon)
    return r, (x * r * gain).astype(jnp.bfloat16)


def norm_backward(x, r, gain, upstream):
    w = upstream * gain
    inner = jnp.mean(w * x, axis=-1, keepdims=True)
    return r * w - x * (r * r * r) * inner


def block_count(length):
    return (length + (ROW_SLOTS - 1)) // ROW_SLOTS


def folded(x):
    return jnp.sum(x.reshape(-1, 8, x.shape[-1]), axis=0)


def causal(keys, rows, first):
    slot = lax.broadcasted_iota(jnp.int32, (keys, rows), 1) & (ROW_SLOTS - 1)
    return lax.broadcasted_iota(jnp.int32, (keys, rows), 0) <= slot + first


def exponent(k, q):
    return jnp.exp2(contract_last(k, q) * (k.shape[-1] ** (-0.5) * LOG2_E))


def before_kernel(
    meta, q_own, g_own, k_own, v_own, q_other, g_other, k_other, v_other, q_gain, k_gain,
    qs, gs, partial,
):
    slots, width = q_own.shape
    head_dim = k_own.shape[1]
    group = width // head_dim
    rows = ROW_SLOTS * group
    gain_q, gain_k = q_gain[...], k_gain[...]
    units = ((q_own, g_own, k_own, v_own), (q_other, g_other, k_other, v_other))
    for which, (q_ref, g_ref, k_ref, v_ref) in enumerate(units):
        length = meta[2 * which]
        _, kn = head_norm(k_ref[...].astype(jnp.float32), gain_k)

        def row_block(b, carry, which=which, q_ref=q_ref, g_ref=g_ref, v_ref=v_ref, kn=kn, length=length):
            first = pl.multiple_of(b * ROW_SLOTS, ROW_SLOTS)
            at = pl.ds(first, ROW_SLOTS)
            out = pl.multiple_of(b * rows, rows)
            live = lax.broadcasted_iota(jnp.int32, (ROW_SLOTS, head_dim), 0) + first < length
            normed, grads = [], []
            for g in range(group):
                cols = slice(g * head_dim, (g + 1) * head_dim)
                normed.append(head_norm(q_ref[at, cols].astype(jnp.float32), gain_q)[1])
                grad = g_ref[at, cols].astype(jnp.float32)
                grads.append(jnp.where(live, grad, 0.0).astype(jnp.bfloat16))
            q, go = jnp.concatenate(normed, axis=0), jnp.concatenate(grads, axis=0)
            qs[0, which, pl.ds(out, rows), :] = q
            gs[0, which, pl.ds(out, rows), :] = go
            e = jnp.where(causal(slots, rows, first), exponent(kn, q), 0.0)
            stats = pl.multiple_of(b * 16, 16)
            partial[0, which, pl.ds(stats, 8), :] = folded(e)
            partial[0, which, pl.ds(stats + 8, 8), :] = folded(e * contract_last(v_ref[...], go))
            return carry

        lax.fori_loop(0, block_count(length), row_block, 0)


def prompt_kernel(
    meta, prompt, qs, gs, partial, ds_out, stats, prompt_grads, e_s, dp_s, dk_acc, dv_acc
):
    total = prompt.shape[0]
    head_dim = qs.shape[-1]
    rows = e_s.shape[1]
    which = pl.program_id(1)
    length, seen = meta[2 * which], meta[2 * which + 1]

    @pl.when(which == 0)
    def _():
        dk_acc[...] = jnp.zeros(dk_acc.shape, jnp.float32)
        dv_acc[...] = jnp.zeros(dv_acc.shape, jnp.float32)

    def blocks(low, high):
        def row_block(b, carry):
            at = pl.ds(pl.multiple_of(b * rows, rows), rows)
            q, go = qs[0, 0, at, :], gs[0, 0, at, :]
            part = pl.multiple_of(b * 16, 16)
            sums = partial[0, 0, pl.ds(part, 8), :]
            dots = partial[0, 0, pl.ds(part + 8, 8), :]
            for base in range(0, high, KEY_CHUNK):
                chunk = slice(base, base + KEY_CHUNK)
                e = exponent(prompt[chunk, :head_dim], q)
                if base + KEY_CHUNK > low:
                    index = lax.broadcasted_iota(jnp.int32, (KEY_CHUNK, rows), 0)
                    e = jnp.where(index < seen - base, e, 0.0)
                dp = contract_last(prompt[chunk, head_dim:], go)
                e_s[chunk] = e
                dp_s[chunk] = dp
                sums += folded(e)
                dots += folded(e * dp)
            inverse = 1.0 / jnp.sum(sums, axis=0, keepdims=True)
            delta = jnp.sum(dots, axis=0, keepdims=True) * inverse
            stats[0, 0, pl.ds(part, 8), :] = jnp.broadcast_to(inverse, (8, rows))
            stats[0, 0, pl.ds(part + 8, 8), :] = jnp.broadcast_to(delta, (8, rows))
            for base in range(0, high, KEY_CHUNK):
                chunk = slice(base, base + KEY_CHUNK)
                p = e_s[chunk] * inverse
                ds = (p * (dp_s[chunk] - delta)).astype(jnp.bfloat16)
                ds_out[0, 0, b, chunk, :] = ds
                dv_acc[chunk] += jnp.dot(
                    p.astype(jnp.bfloat16), go, preferred_element_type=jnp.float32
                )
                dk_acc[chunk] += jnp.dot(ds, q, preferred_element_type=jnp.float32)
            return carry

        lax.fori_loop(0, block_count(length), row_block, 0)

    step = total // KEY_STEPS
    for n in range(1, KEY_STEPS + 1):
        low, high = (n - 1) * step, n * step
        pl.when((seen > low) & (seen <= high))(functools.partial(blocks, low, high))

    @pl.when(which == pl.num_programs(1) - 1)
    def _():
        scale = head_dim ** (-0.5)
        prompt_grads[:, :head_dim] = (dk_acc[...] * scale).astype(jnp.bfloat16)
        prompt_grads[:, head_dim:] = dv_acc[...].astype(jnp.bfloat16)


def after_kernel(
    meta, q_own, k_own, v_own, q_other, k_other, v_other, prompt, qs, gs, ds_in, stats,
    q_gain, k_gain,
    dq_own, dk_own, dv_own, dq_other, dk_other, dv_other, dk_acc, dv_acc,
):
    slots, width = q_own.shape
    head_dim = k_own.shape[1]
    group = width // head_dim
    rows = ROW_SLOTS * group
    total = prompt.shape[0]
    scale = head_dim ** (-0.5)
    gain_q, gain_k = q_gain[...], k_gain[...]
    units = (
        (q_own, k_own, v_own, dq_own, dk_own, dv_own),
        (q_other, k_other, v_other, dq_other, dk_other, dv_other),
    )
    for which, (q_ref, k_ref, v_ref, dq_ref, dk_ref, dv_ref) in enumerate(units):
        length, seen = meta[2 * which], meta[2 * which + 1]
        key_x = k_ref[...].astype(jnp.float32)
        key_r, kn = head_norm(key_x, gain_k)
        dq_ref[...] = jnp.zeros(dq_ref.shape, dq_ref.dtype)
        dk_acc[...] = jnp.zeros(dk_acc.shape, jnp.float32)
        dv_acc[...] = jnp.zeros(dv_acc.shape, jnp.float32)

        def blocks(high, which=which, q_ref=q_ref, v_ref=v_ref, dq_ref=dq_ref, kn=kn, length=length):
            def row_block(b, carry):
                first = pl.multiple_of(b * ROW_SLOTS, ROW_SLOTS)
                at = pl.ds(pl.multiple_of(b * rows, rows), rows)
                q, go = qs[0, which, at, :], gs[0, which, at, :]
                part = pl.multiple_of(b * 16, 16)
                inverse = stats[0, which, pl.ds(part, 8), :][:1]
                delta = stats[0, which, pl.ds(part + 8, 8), :][:1]
                e = jnp.where(causal(slots, rows, first), exponent(kn, q), 0.0)
                p = e * inverse
                ds = (p * (contract_last(v_ref[...], go) - delta)).astype(jnp.bfloat16)
                dv_acc[...] += jnp.dot(
                    p.astype(jnp.bfloat16), go, preferred_element_type=jnp.float32
                )
                dk_acc[...] += jnp.dot(ds, q, preferred_element_type=jnp.float32)
                dq = contract_first(ds, kn) + contract_first(
                    ds_in[0, which, b, :high, :], prompt[:high, :head_dim]
                )
                dq = dq * scale
                for g in range(group):
                    cols = slice(g * head_dim, (g + 1) * head_dim)
                    x = q_ref[pl.ds(first, ROW_SLOTS), cols].astype(jnp.float32)
                    r = lax.rsqrt(jnp.mean(x * x, axis=-1, keepdims=True) + epsilon)
                    up = dq[g * ROW_SLOTS : (g + 1) * ROW_SLOTS]
                    dx = norm_backward(x, r, gain_q, up)
                    dq_ref[pl.ds(first, ROW_SLOTS), cols] = dx.astype(jnp.bfloat16)
                return carry

            lax.fori_loop(0, block_count(length), row_block, 0)

        step = total // KEY_STEPS
        for n in range(1, KEY_STEPS + 1):
            low, high = (n - 1) * step, n * step
            pl.when((seen > low) & (seen <= high))(functools.partial(blocks, high))
        dk = norm_backward(key_x, key_r, gain_k, dk_acc[...] * scale)
        dk_ref[...] = dk.astype(jnp.bfloat16)
        dv_ref[...] = dv_acc[...].astype(jnp.bfloat16)


def attend(heads, meta, own, other, prompt, weight_pair, q_gain, k_gain, width, head_dim):
    slots, total = own.shape[0], prompt.shape[0]
    group = width // head_dim
    rows = ROW_SLOTS * group
    steps = slots // ROW_SLOTS
    narrow = 2 * heads * group
    low, high = jnp.bfloat16, jnp.float32
    scalars = pl.BlockSpec(memory_space=pltpu.SMEM)
    gain = pl.BlockSpec((1, head_dim), lambda *i: (0, 0))

    def columns(block, index):
        return pl.BlockSpec((slots, block), lambda i, index=index: (0, index + i))

    def by_head(rows, block):
        return pl.BlockSpec((rows, block), lambda i, *_: (0, i))

    def by_pair(*shape):
        return pl.BlockSpec((1, 2, *shape), lambda i: (i, 0) + (0,) * len(shape))

    def by_unit(*shape):
        return pl.BlockSpec((1, 1, *shape), lambda i, k: (i, k) + (0,) * len(shape))

    def cost(products, keys, moved):
        return pl.CostEstimate(
            flops=heads * 2 * products * 2 * slots * group * keys * head_dim,
            bytes_accessed=moved,
            transcendentals=heads * 2 * slots * group * keys,
        )

    q_side = columns(width, 0)
    g_side = columns(width, heads)
    k_side = columns(head_dim, narrow)
    v_side = columns(head_dim, narrow + heads)
    stack, stat, shade = (steps * rows, head_dim), (steps * 16, rows), (steps, total, rows)

    def limit(mebibytes):
        return pltpu.CompilerParams(vmem_limit_bytes=mebibytes * 1024 * 1024)

    def shaped(shape, kind):
        return jax.ShapeDtypeStruct((heads, 2, *shape), kind)

    qs, gs, partial = pl.pallas_call(
        before_kernel,
        grid=(heads,),
        in_specs=[scalars, q_side, g_side, k_side, v_side, q_side, g_side, k_side, v_side, gain, gain],
        out_specs=[by_pair(*stack), by_pair(*stack), by_pair(*stat)],
        out_shape=[shaped(stack, low), shaped(stack, low), shaped(stat, high)],
        compiler_params=limit(8),
        cost_estimate=cost(2, slots, 4 * 1024 * 1024),
    )(meta, own, own, own, own, other, other, other, other, q_gain, k_gain)
    weight_pair, prompt, qs, gs, partial = lax.optimization_barrier(
        (weight_pair, prompt, qs, gs, partial)
    )
    weight = from_everyone(weight_pair, FAR).reshape(-1, weight_pair.shape[1])
    ds, stats, prompt_grads = pl.pallas_call(
        prompt_kernel,
        grid=(heads, 2),
        in_specs=[scalars, by_head(total, 2 * head_dim), by_unit(*stack), by_unit(*stack), by_unit(*stat)],
        out_specs=[by_unit(*shade), by_unit(*stat), by_head(total, 2 * head_dim)],
        out_shape=[
            shaped(shade, low),
            shaped(stat, high),
            jax.ShapeDtypeStruct((total, heads * 2 * head_dim), low),
        ],
        scratch_shapes=[
            pltpu.VMEM((total, rows), high),
            pltpu.VMEM((total, rows), high),
            pltpu.VMEM((total, head_dim), high),
            pltpu.VMEM((total, head_dim), high),
        ],
        compiler_params=limit(57),
        cost_estimate=cost(4, total, 12 * 1024 * 1024),
    )(meta, prompt, qs, gs, partial)
    outs = [(slots, width), (slots, head_dim), (slots, head_dim)] * 2
    grads = pl.pallas_call(
        after_kernel,
        grid=(heads,),
        in_specs=[scalars, q_side, k_side, v_side, q_side, k_side, v_side]
        + [by_head(total, 2 * head_dim), by_pair(*stack), by_pair(*stack)]
        + [by_pair(*shade), by_pair(*stat), gain, gain],
        out_specs=[by_head(*s) for s in outs],
        out_shape=[jax.ShapeDtypeStruct((n, heads * m), low) for n, m in outs],
        scratch_shapes=[pltpu.VMEM((slots, head_dim), high), pltpu.VMEM((slots, head_dim), high)],
        compiler_params=limit(57),
        cost_estimate=cost(2, total, 14 * 1024 * 1024),
    )(meta, own, own, own, other, other, other, prompt, qs, gs, ds, stats, q_gain, k_gain)
    return (*grads, prompt_grads, weight)


def on_device(
    prompt_key_rows,
    prompt_value_rows,
    queries,
    keys,
    values,
    output_gradient,
    lengths,
    prompt_visible_rows,
    query_gain,
    key_norm_gain,
    key_value_weight,
):
    head_dim = query_gain.shape[0]
    core = lax.axis_index(PAIR)
    cores = lax.axis_size(PAIR)
    heads = keys.shape[1] // head_dim // cores
    narrow = heads * head_dim
    wide = queries.shape[1] // cores
    width = wide // heads
    near, far = lax.axis_size(NEAR), lax.axis_size(FAR)
    q_gain, k_gain = query_gain[None, :], key_norm_gain[None, :]

    def part(a, which, n):
        return lax.dynamic_slice_in_dim(a, which * n, n, axis=1)

    def in_core_order(mine, theirs):
        flip = core == 0
        return jnp.where(flip, mine, theirs), jnp.where(flip, theirs, mine)

    def prompt_part(which):
        return jnp.concatenate(
            [part(prompt_key_rows, which, narrow), part(prompt_value_rows, which, narrow)], axis=1
        )

    def pack(which):
        return jnp.concatenate(
            [
                part(queries, which, wide),
                part(output_gradient, which, wide),
                part(keys, which, narrow),
                part(values, which, narrow),
            ],
            axis=1,
        )

    def weight_part(which):
        cut = key_value_weight.reshape(-1, 2, cores, heads, head_dim)
        cut = lax.dynamic_index_in_dim(cut, which, 2, keepdims=False)
        return cut.transpose(0, 2, 1, 3).reshape(-1, 2 * narrow)

    raw = jnp.concatenate(in_core_order(prompt_part(core), swap(prompt_part(1 - core))), axis=0)
    count = raw.shape[0]
    px = raw[:, :narrow].astype(jnp.float32).reshape(count, heads, head_dim)
    pr = lax.rsqrt(jnp.mean(px * px, axis=-1, keepdims=True) + epsilon)
    pn = (px * pr * key_norm_gain).astype(jnp.bfloat16).reshape(count, narrow)
    pv = raw[:, narrow:]

    meta_own = jnp.stack([lengths[0], prompt_visible_rows[0]])
    meta = jnp.concatenate([meta_own, swap(meta_own)])
    own, other = pack(core), swap(pack(1 - core))
    weight_pair = jnp.concatenate(
        in_core_order(weight_part(core), swap(weight_part(1 - core))), axis=0
    )

    both = jnp.concatenate(
        [
            a[:, h * head_dim : (h + 1) * head_dim]
            for h in range(heads)
            for a in (pn, pv)
        ],
        axis=1,
    )
    prompt = from_everyone(both, PLANE).reshape(-1, 2 * narrow)

    results = attend(
        heads, meta, own, other, prompt, weight_pair, q_gain, k_gain, width, head_dim
    )

    sent, weight = lax.optimization_barrier((results[6], results[7]))
    sent = sent.reshape(far * near, count, 2 * narrow)
    parts = lax.all_to_all(sent, PLANE, 0, 0, tiled=True)
    total = jnp.sum(parts.astype(jnp.float32), axis=0).reshape(count, heads, 2, head_dim)
    w = total[:, :, 0] * key_norm_gain
    inner = jnp.mean(w * px, axis=-1, keepdims=True)
    dk = pr * w - px * (pr * pr * pr) * inner
    grads = jnp.stack([dk, total[:, :, 1]], axis=2).reshape(count, 2 * narrow)
    rows = from_everyone(grads.astype(jnp.bfloat16), NEAR).reshape(-1, 2 * narrow)

    def assembled(index):
        return jnp.concatenate(in_core_order(results[index], swap(results[index + 3])), axis=1)

    query_grad, key_grad, value_grad = assembled(0), assembled(1), assembled(2)

    hidden = contract_last(rows, weight)
    per_core = count // cores
    hidden = hidden.reshape(near, cores, per_core, -1)
    mine = lax.dynamic_index_in_dim(hidden, core, 1, keepdims=False)
    theirs = lax.dynamic_index_in_dim(hidden, 1 - core, 1, keepdims=False)
    mine = (mine + swap(theirs.astype(jnp.bfloat16)).astype(jnp.float32)).astype(jnp.bfloat16)
    arrived = lax.all_to_all(mine, NEAR, 0, 0, tiled=True)
    arrived = arrived.reshape(near, per_core, far, -1)
    hidden_grad = arrived.transpose(1, 2, 0, 3).reshape(per_core, -1)
    return (query_grad, key_grad, value_grad, hidden_grad)


def solution(mesh):
    finer = Mesh(
        mesh.devices.reshape(mesh.shape["grp"], 8, 8, 2), ("grp", "cand_0", "cand_1", "cand_2")
    )
    return jax.shard_map(
        on_device,
        mesh=finer,
        in_specs=(
            P(GRP_CAND, None),
            P(GRP_CAND, None),
            P(GRP_CAND, None),
            P(GRP_CAND, None),
            P(GRP_CAND, None),
            P(GRP_CAND, None),
            P(GRP_CAND),
            P(GRP_CAND),
            P(),
            P(),
            P(CAND, None),
        ),
        out_specs=(P(GRP_CAND, None), P(GRP_CAND, None), P(GRP_CAND, None), P(GRP_CAND, None)),
        check_vma=False,
    )
```

time: 175 us -> 151 us (0.86)
  waiting for transfers between devices: 68.8 us -> 42.7 us
  starting transfers between devices: 74 us -> 56.9 us
  Pallas kernels: 8.34 us -> 25 us
  other arithmetic: 9.74 us -> 11.5 us
    all_to_all x1, starting transfers between devices: 26.1 us -> 6.69 us  [on_device(): parts = lax.all_to_all(sent, PLANE, 0, 0, tiled=True)]
    pallas_call x1 -> x3, Pallas kernels: 8.34 us -> 25 us  [the longest x1 11.1 us: attend(): pl.pallas_call(prompt_kernel, grid=(heads, 2), in_specs=[scalars, by_head...]
    all_to_all x3, waiting for transfers between devices: 39.2 us -> 25.8 us  [from_everyone(): return lax.all_to_all(copies, axis, split_axis=0, concat_axis=0, tiled=True)]
    all_to_all x1, waiting for transfers between devices: 21.6 us -> 9.76 us  [on_device(): parts = lax.all_to_all(sent, PLANE, 0, 0, tiled=True)]
    concatenate x2, other arithmetic: 0.16 us -> 2.4 us  [pack(): jnp.concatenate([part(queries, which, wide), part(output_gradient, which,...]
  transfers between devices with their start and end apart: 13 -> 13, of which waited for: 9 -> 8; matrix products, arithmetic and copies ran while one was open for 8% -> 10% of each run, Pallas kernels for 0% -> 17%
where the time goes in v1:
time: 151 us; the launch traced here: 150 us
  starting transfers between devices  56.9 us (38%)
  waiting for transfers between devices  42.7 us (28%)
  Pallas kernels  25 us (17%)
  other arithmetic  11.5 us (8%)
  local copies, waits for them, and re-layouts  11 us (7%)
  between operations  2.39 us (2%)
    ppermute x8, starting transfers between devices, swap(): return lax.ppermute(x, PAIR, [(0, 1), (1, 0)])  28.7 us
    all_to_all x3, waiting for transfers between devices, from_everyone(): return lax.all_to_all(copies, axis, split_axis=0, concat_axis=0, tiled=True)  25.8 us
    all_to_all x3, starting transfers between devices, from_everyone(): return lax.all_to_all(copies, axis, split_axis=0, concat_axis=0, tiled=True)  18 us
    pallas_call x1, Pallas kernels, attend(): pl.pallas_call(prompt_kernel, grid=(heads, 2), in_specs=[scalars, by_head...  11.1 us
    pallas_call x1, Pallas kernels, attend(): pl.pallas_call(after_kernel, grid=(heads,), in_specs=[scalars, q_side, k_...  10.4 us
    all_to_all x1, waiting for transfers between devices, on_device(): parts = lax.all_to_all(sent, PLANE, 0, 0, tiled=True)  9.76 us
    all_to_all x1, starting transfers between devices, on_device(): parts = lax.all_to_all(sent, PLANE, 0, 0, tiled=True)  6.69 us
    all_to_all x1, waiting for transfers between devices, on_device(): arrived = lax.all_to_all(mine, NEAR, 0, 0, tiled=True)  6.1 us
  transfers between devices with their start and end apart: 13, of which 8 were waited for; matrix products, arithmetic and copies ran while one was open for 10% of the time, Pallas kernels for 17%

profile of v1, /device:TPU:513, one launch (start us, length us, event | category | flops | bytes accessed | tf_op | source)
XLA Modules:
  0.0 149.9 jit_solution(5192252135858171171)
XLA Ops:
  0.7 0.9 constant_dynamic-slice_fusion.2
  1.5 20.4 %collective-permute-start.3 = (bf16[8,512]{1,0:T(8,128)(2,1)S(1)}, bf16[8,512]{1,0:T(8,128)(2,1)S(1)}, u32[]{:S(2)}, u32[]{:S(2)}) collective-permute-start(bf16[8,512]{1,0:T(8,128)(2,1)S(1)} %pad_maximum_fusion.8), channel_id=1, source_target_pairs={{0,1},{1,0},{2,3},{3,2},{4,5},{5,4},{6,7},{7,6},{8,9},{9,8},{10,11... | collective-permute-start | bytes 24584 | tf_op jit(solution)/shard_map/ppermute | solution.py:24
  22.0 0.7 broadcast_bitcast_fusion
  22.6 0.2 collective-permute-done.3
  22.9 0.1 multiply_reduce_fusion.1
  22.9 0.6 multiply_multiply_fusion
  23.6 0.1 mul.123
  23.7 1.1 broadcast_in_dim.19
  24.8 6.5 %all-to-all-start = ((bf16[64,16,512]{2,1,0:T(8,128)(2,1)}), bf16[64,16,512]{2,1,0:T(8,128)(2,1)S(1)}, u32[]{:S(2)}, u32[]{:S(2)}) async-start(bf16[64,16,512]{2,1,0:T(8,128)(2,1)} %broadcast_in_dim.19), calls=%async_computation | async-start | bytes 2097152 | tf_op jit(solution)/shard_map/all_to_all | solution.py:29
  31.3 0.0 copy-start.18
  31.3 0.0 copy-start.19
  31.3 1.1 constant_dynamic-slice_fusion.8
  32.5 1.1 pad_maximum_fusion.1
  33.6 0.3 collective-permute-start.1
  35.3 0.6 pad_add_fusion
  35.9 0.2 collective-permute-start
  36.1 0.1 constant_dynamic-slice_fusion.5
  36.2 0.6 reshape.85
  36.8 0.3 collective-permute-start.2
  37.2 0.6 reshape.84
  37.8 1.3 pad_maximum_fusion.q_own.g_own.k_own.v_own
  39.1 0.0 collective-permute-done
  39.1 0.7 pad_add_fusion.1.meta
  39.8 0.0 collective-permute-done.2
  39.8 0.8 broadcast_select_fusion.7
  40.6 0.0 collective-permute-done.1.q_other.g_other.k_other.v_other
  40.7 3.6 %shard_map.138 = (bf16[2,2,1024,128]{3,2,1,0:T(8,128)(2,1)S(1)}, bf16[2,2,1024,128]{3,2,1,0:T(8,128)(2,1)S(1)}, f32[2,2,64,256]{3,2,1,0:T(8,128)S(1)}) custom-call(s32[4]{0:T(128)S(1)} %pad_add_fusion.1.meta, bf16[128,4608]{1,0:T(8,128)(2,1)S(1)} %pad_maximum_fusion.q_own.g_own.k_own.v_own, bf16[128,4608]{1,0:T(8,128)(2,1)S(1)} %pad_maximum_fusion.q_own.g_own.k_own.v_own, ...), custom_call_target="tpu_custom_call" | custom-call | flops 268435456 | bytes 4194304 | tf_op jit(solution)/shard_map/pallas_call | solution.py:274
  44.3 1.0 copy-done.2
  45.4 1.0 copy-done.3
  46.3 0.7 copy-done.8
  47.0 10.8 %all-to-all-done = bf16[64,16,512]{2,1,0:T(8,128)(2,1)S(1)} async-done(((bf16[64,16,512]{2,1,0:T(8,128)(2,1)}), bf16[64,16,512]{2,1,0:T(8,128)(2,1)S(1)}, u32[]{:S(2)}, u32[]{:S(2)}) %all-to-all-start) | async-done | bytes 1048608 | tf_op jit(solution)/shard_map/all_to_all | solution.py:29
  57.8 1.0 broadcast_in_dim.22
  58.8 6.3 %all-to-all-start.1 = ((bf16[8,80,512]{2,1,0:T(8,128)(2,1)}), bf16[8,80,512]{2,1,0:T(8,128)(2,1)S(1)}, u32[]{:S(2)}, u32[]{:S(2)}) async-start(bf16[8,80,512]{2,1,0:T(8,128)(2,1)} %broadcast_in_dim.22), calls=%async_computation.1 | async-start | bytes 1310720 | tf_op jit(solution)/shard_map/all_to_all | solution.py:29
  65.1 11.1 %shard_map.139 = (bf16[2,2,4,1024,256]{4,3,2,1,0:T(8,128)(2,1)}, f32[2,2,64,256]{3,2,1,0:T(8,128)}, bf16[1024,512]{1,0:T(8,128)(2,1)}) custom-call(s32[4]{0:T(128)} %copy-done.6, bf16[1024,512]{1,0:T(8,128)(2,1)} %bitcast.46, bf16[2,2,1024,128]{3,2,1,0:T(8,128)(2,1)} %copy-done.2, bf16[2,2,1024,128]{3,2,1,0:T(8,128)(2,1)} %copy-done.3, ...), custom_call_target="tpu_custom_call" | custom-call | flops 4294967296 | bytes 12582912 | tf_op jit(solution)/shard_map/pallas_call | solution.py:287
  76.2 8.4 %all-to-all-done.1 = bf16[8,80,512]{2,1,0:T(8,128)(2,1)S(1)} async-done(((bf16[8,80,512]{2,1,0:T(8,128)(2,1)}), bf16[8,80,512]{2,1,0:T(8,128)(2,1)S(1)}, u32[]{:S(2)}, u32[]{:S(2)}) %all-to-all-start.1) | async-done | bytes 655392 | tf_op jit(solution)/shard_map/all_to_all | solution.py:29
  84.6 6.7 %all-to-all-start.2 = ((bf16[64,16,512]{2,1,0:T(8,128)(2,1)}), bf16[64,16,512]{2,1,0:T(8,128)(2,1)S(1)}, u32[]{:S(2)}, u32[]{:S(2)}) async-start(bf16[64,16,512]{2,1,0:T(8,128)(2,1)} %bitcast.49), calls=%async_computation.2 | async-start | bytes 2097152 | tf_op jit(solution)/shard_map/all_to_all | solution.py:403
  91.3 0.0 copy-start.5
  91.3 10.4 %shard_map.140 = (bf16[128,2048]{1,0:T(8,128)(2,1)}, bf16[128,256]{1,0:T(8,128)(2,1)}, bf16[128,256]{1,0:T(8,128)(2,1)}, bf16[128,2048]{1,0:T(8,128)(2,1)}, bf16...) custom-call(s32[4]{0:T(128)} %copy-done.6, bf16[128,4608]{1,0:T(8,128)(2,1)} %copy-done, bf16[128,4608]{1,0:T(8,128)(2,1)} %copy-done, ...), custom_call_target="tpu_custom_call" | custom-call | flops 2147483648 | bytes 14680064 | tf_op jit(solution)/shard_map/pallas_call | solution.py:307
  101.7 1.9 %collective-permute-start.5 = (bf16[128,256]{1,0:T(8,128)(2,1)}, bf16[128,256]{1,0:T(8,128)(2,1)S(1)}, u32[]{:S(2)}, u32[]{:S(2)}) collective-permute-start(bf16[128,256]{1,0:T(8,128)(2,1)} %get-tuple-element.35), channel_id=1, source_target_pairs={{0,1},{1,0},{2,3},{3,2},{4,5},{5,4},{6,7},{7,6},{8,9},{9,8},{10,11... | collective-permute-start | bytes 196616 | tf_op jit(solution)/shard_map/ppermute | solution.py:24
  103.7 0.2 collective-permute-start.4
  103.8 0.5 collective-permute-start.6
  104.3 0.4 collective-permute-done.5
  104.8 0.9 broadcast_select_fusion.5
  105.6 0.4 collective-permute-done.6
  106.0 0.9 broadcast_select_fusion.3
  106.9 9.8 %all-to-all-done.2 = bf16[64,16,512]{2,1,0:T(8,128)(2,1)S(1)} async-done(((bf16[64,16,512]{2,1,0:T(8,128)(2,1)}), bf16[64,16,512]{2,1,0:T(8,128)(2,1)S(1)}, u32[]{:S(2)}, u32[]{:S(2)}) %all-to-all-start.2) | async-done | bytes 1048608 | tf_op jit(solution)/shard_map/all_to_all | solution.py:403
  116.7 0.2 convert_reduce_fusion
  116.9 0.1 multiply_reduce_fusion
  117.1 0.2 subtract_convert_fusion
  117.3 0.7 broadcast_in_dim.23
  118.0 5.1 %all-to-all-start.3 = ((bf16[8,16,512]{2,1,0:T(8,128)(2,1)}), bf16[8,16,512]{2,1,0:T(8,128)(2,1)S(1)}, u32[]{:S(2)}, u32[]{:S(2)}) async-start(bf16[8,16,512]{2,1,0:T(8,128)(2,1)} %broadcast_in_dim.23), calls=%async_computation.3 | async-start | bytes 262144 | tf_op jit(solution)/shard_map/all_to_all | solution.py:29
  123.1 0.7 pad_maximum_fusion.3
  123.8 0.7 pad_maximum_fusion.4
  124.4 6.6 %all-to-all-done.3 = bf16[8,16,512]{2,1,0:T(8,128)(2,1)S(1)} async-done(((bf16[8,16,512]{2,1,0:T(8,128)(2,1)}), bf16[8,16,512]{2,1,0:T(8,128)(2,1)S(1)}, u32[]{:S(2)}, u32[]{:S(2)}) %all-to-all-start.3) | async-done | bytes 131104 | tf_op jit(solution)/shard_map/all_to_all | solution.py:29
  131.0 0.3 fusion
  131.4 4.8 %collective-permute-start.7 = (bf16[8,8,640]{2,1,0:T(8,128)(2,1)S(1)}, bf16[8,8,640]{2,1,0:T(8,128)(2,1)S(1)}, u32[]{:S(2)}, u32[]{:S(2)}) collective-permute-start(bf16[8,8,640]{2,1,0:T(8,128)(2,1)S(1)} %fusion.4), channel_id=1, source_target_pairs={{0,1},{1,0},{2,3},{3,2},{4,5},{5,4},{6,7},{7,6},{8,9},{9,8},{10,11... | collective-permute-start | bytes 245768 | tf_op jit(solution)/shard_map/ppermute | solution.py:24
  136.3 1.1 broadcast_select_fusion.1
  137.4 0.7 fusion.2
  138.0 3.6 %all-to-all-start.4 = ((bf16[8,8,640]{2,1,0:T(8,128)(2,1)}), bf16[8,8,640]{2,1,0:T(8,128)(2,1)S(1)}, u32[]{:S(2)}, u32[]{:S(2)}) async-start(bf16[8,8,640]{2,1,0:T(8,128)(2,1)} %fusion.2), calls=%async_computation.4 | async-start | bytes 163840 | tf_op jit(solution)/shard_map/all_to_all | solution.py:422
  141.6 1.0 pad_maximum_fusion.2
  142.7 6.1 %all-to-all-done.4 = bf16[8,8,640]{2,1,0:T(8,128)(2,1)S(1)} async-done(((bf16[8,8,640]{2,1,0:T(8,128)(2,1)}), bf16[8,8,640]{2,1,0:T(8,128)(2,1)S(1)}, u32[]{:S(2)}, u32[]{:S(2)}) %all-to-all-start.4) | async-done | bytes 81952 | tf_op jit(solution)/shard_map/all_to_all | solution.py:422
  148.8 0.2 reshape.92
  148.9 0.1 copy.18
  149.0 0.8 reshape.93
  (61 shorter events, 0.4 us)
Async XLA Ops:
  0.6 30.7 %copy-start.10 = (bf16[128,4096]{1,0:T(8,128)(2,1)S(1)}, bf16[128,4096]{1,0:T(8,128)(2,1)}, u32[]{:S(2)}) copy-start(bf16[128,4096]{1,0:T(8,128)(2,1)} %param.16) | copy-start | bytes 3145732
  0.6 30.7 %copy-start.11 = (bf16[128,4096]{1,0:T(8,128)(2,1)S(1)}, bf16[128,4096]{1,0:T(8,128)(2,1)}, u32[]{:S(2)}) copy-start(bf16[128,4096]{1,0:T(8,128)(2,1)} %param.13) | copy-start | bytes 3145732
  1.5 21.2 %collective-permute-start.3 = (bf16[8,512]{1,0:T(8,128)(2,1)S(1)}, bf16[8,512]{1,0:T(8,128)(2,1)S(1)}, u32[]{:S(2)}, u32[]{:S(2)}) collective-permute-start(bf16[8,512]{1,0:T(8,128)(2,1)S(1)} %pad_maximum_fusion.8), channel_id=1, source_target_pairs={{0,1},{1,0},{2,3},{3,2},{4,5},{5,4},{6,7},{7,6},{8,9},{9,8},{10,11... | collective-permute-start | bytes 24584 | tf_op jit(solution)/shard_map/ppermute | solution.py:24
  22.8 2.0 %copy-start.14 = (f32[16,256]{1,0:T(8,128)}, f32[16,256]{1,0:T(8,128)S(1)}, u32[]{:S(2)}) copy-start(f32[16,256]{1,0:T(8,128)S(1)} %fusion.12) | copy-start | bytes 49156
  22.8 1.9 %copy-start.16 = (f32[16,2,128]{2,1,0:T(2,128)}, f32[16,2,128]{2,1,0:T(2,128)S(1)}, u32[]{:S(2)}) copy-start(f32[16,2,128]{2,1,0:T(2,128)S(1)} %reshape.86) | copy-start | bytes 49156
  24.8 33.0 %all-to-all-start = ((bf16[64,16,512]{2,1,0:T(8,128)(2,1)}), bf16[64,16,512]{2,1,0:T(8,128)(2,1)S(1)}, u32[]{:S(2)}, u32[]{:S(2)}) async-start(bf16[64,16,512]{2,1,0:T(8,128)(2,1)} %broadcast_in_dim.19), calls=%async_computation | async-start | bytes 2097152 | tf_op jit(solution)/shard_map/all_to_all | solution.py:29
  31.3 1.2 copy-start.18
  31.3 1.1 copy-start.19
  32.5 3.6 %copy-start.20 = (bf16[40,1024]{1,0:T(8,128)(2,1)S(1)}, bf16[40,1024]{1,0:T(8,128)(2,1)}, u32[]{:S(2)}) copy-start(bf16[40,1024]{1,0:T(8,128)(2,1)} %param.21) | copy-start | bytes 245764
  33.6 7.0 %copy-start.4 = (f32[128]{0:T(128)S(1)}, f32[128]{0:T(128)}, u32[]{:S(2)}) copy-start(f32[128]{0:T(128)} %param.20) | copy-start | bytes 1540
  33.6 7.0 %copy-start.7 = (f32[128]{0:T(128)S(1)}, f32[128]{0:T(128)}, u32[]{:S(2)}) copy-start(f32[128]{0:T(128)} %param.19) | copy-start | bytes 1540
  33.6 7.0 %collective-permute-start.1 = (bf16[128,4608]{1,0:T(8,128)(2,1)}, bf16[128,4608]{1,0:T(8,128)(2,1)S(1)}, u32[]{:S(2)}, u32[]{:S(2)}) collective-permute-start(bf16[128,4608]{1,0:T(8,128)(2,1)} %pad_maximum_fusion.1), channel_id=1, source_target_pairs={{0,1},{1,0},{2,3},{3,2},{4,5},{5,4},{6,7},{7,6},{8,9},{9,8},{10,11... | collective-permute-start | bytes 3538952 | tf_op jit(solution)/shard_map/ppermute | solution.py:24
  35.9 3.3 %collective-permute-start = (s32[2]{0:T(128)}, s32[2]{0:T(128)}, u32[]{:S(2)}, u32[]{:S(2)}) collective-permute-start(s32[2]{0:T(128)} %pad_add_fusion), channel_id=1, source_target_pairs={{0,1},{1,0},{2,3},{3,2},{4,5},{5,4},{6,7},{7,6},{8,9},{9,8},{10,11... | collective-permute-start | bytes 32 | tf_op jit(solution)/shard_map/ppermute | solution.py:24
  36.8 3.0 %collective-permute-start.2 = (bf16[40,512]{1,0:T(8,128)(2,1)}, bf16[40,512]{1,0:T(8,128)(2,1)}, u32[]{:S(2)}, u32[]{:S(2)}) collective-permute-start(bf16[40,512]{1,0:T(8,128)(2,1)} %reshape.85), channel_id=1, source_target_pairs={{0,1},{1,0},{2,3},{3,2},{4,5},{5,4},{6,7},{7,6},{8,9},{9,8},{10,11... | collective-permute-start | bytes 122888 | tf_op jit(solution)/shard_map/ppermute | solution.py:24
  37.8 2.0 %copy-start.13 = (bf16[40,512]{1,0:T(8,128)(2,1)S(1)}, bf16[40,512]{1,0:T(8,128)(2,1)}, u32[]{:S(2)}) copy-start(bf16[40,512]{1,0:T(8,128)(2,1)} %reshape.84) | copy-start | bytes 122884
  39.1 5.2 %copy-start = (bf16[128,4608]{1,0:T(8,128)(2,1)}, bf16[128,4608]{1,0:T(8,128)(2,1)S(1)}, u32[]{:S(2)}) copy-start(bf16[128,4608]{1,0:T(8,128)(2,1)S(1)} %pad_maximum_fusion.q_own.g_own.k_own.v_own) | copy-start | bytes 3538948
  39.8 4.5 %copy-start.6 = (s32[4]{0:T(128)}, s32[4]{0:T(128)S(1)}, u32[]{:S(2)}) copy-start(s32[4]{0:T(128)S(1)} %pad_add_fusion.1.meta) | copy-start | bytes 52
  40.6 3.7 %copy-start.1 = (bf16[128,4608]{1,0:T(8,128)(2,1)}, bf16[128,4608]{1,0:T(8,128)(2,1)S(1)}, u32[]{:S(2)}) copy-start(bf16[128,4608]{1,0:T(8,128)(2,1)S(1)} %collective-permute-done.1.q_other.g_other.k_other.v_other) | copy-start | bytes 3538948
  44.3 1.0 copy-start.2
  45.4 1.0 copy-start.3
  46.3 0.7 copy-start.8
  57.8 7.3 %copy-start.9 = (bf16[64,16,512]{2,1,0:T(8,128)(2,1)}, bf16[64,16,512]{2,1,0:T(8,128)(2,1)S(1)}, u32[]{:S(2)}) copy-start(bf16[64,16,512]{2,1,0:T(8,128)(2,1)S(1)} %all-to-all-done) | copy-start | bytes 3145732
  58.8 25.8 %all-to-all-start.1 = ((bf16[8,80,512]{2,1,0:T(8,128)(2,1)}), bf16[8,80,512]{2,1,0:T(8,128)(2,1)S(1)}, u32[]{:S(2)}, u32[]{:S(2)}) async-start(bf16[8,80,512]{2,1,0:T(8,128)(2,1)} %broadcast_in_dim.22), calls=%async_computation.1 | async-start | bytes 1310720 | tf_op jit(solution)/shard_map/all_to_all | solution.py:29
  84.6 32.1 %all-to-all-start.2 = ((bf16[64,16,512]{2,1,0:T(8,128)(2,1)}), bf16[64,16,512]{2,1,0:T(8,128)(2,1)S(1)}, u32[]{:S(2)}, u32[]{:S(2)}) async-start(bf16[64,16,512]{2,1,0:T(8,128)(2,1)} %bitcast.49), calls=%async_computation.2 | async-start | bytes 2097152 | tf_op jit(solution)/shard_map/all_to_all | solution.py:403
  91.3 12.4 %copy-start.15 = (f32[16,256]{1,0:T(8,128)S(1)}, f32[16,256]{1,0:T(8,128)}, u32[]{:S(2)}) copy-start(f32[16,256]{1,0:T(8,128)} %copy-done.14) | copy-start | bytes 49156
  91.3 25.6 %copy-start.5 = (f32[128]{0:T(128)S(1)}, f32[128]{0:T(128)}, u32[]{:S(2)}) copy-start(f32[128]{0:T(128)} %param.20) | copy-start | bytes 1540
  91.3 25.6 %copy-start.17 = (f32[16,2,128]{2,1,0:T(2,128)S(1)}, f32[16,2,128]{2,1,0:T(2,128)}, u32[]{:S(2)}) copy-start(f32[16,2,128]{2,1,0:T(2,128)} %copy-done.16) | copy-start | bytes 49156
  91.3 25.7 %copy-start.21 = (f32[16,2]{1,0:T(8,128)S(1)}, f32[16,2]{1,0:T(8,128)}, u32[]{:S(2)}) copy-start(f32[16,2]{1,0:T(8,128)} %get-tuple-element.62) | copy-start | bytes 388
  101.7 3.0 %collective-permute-start.5 = (bf16[128,256]{1,0:T(8,128)(2,1)}, bf16[128,256]{1,0:T(8,128)(2,1)S(1)}, u32[]{:S(2)}, u32[]{:S(2)}) collective-permute-start(bf16[128,256]{1,0:T(8,128)(2,1)} %get-tuple-element.35), channel_id=1, source_target_pairs={{0,1},{1,0},{2,3},{3,2},{4,5},{5,4},{6,7},{7,6},{8,9},{9,8},{10,11... | collective-permute-start | bytes 196616 | tf_op jit(solution)/shard_map/ppermute | solution.py:24
  103.7 32.6 %copy-start.12 = (bf16[128,2048]{1,0:T(8,128)(2,1)S(1)}, bf16[128,2048]{1,0:T(8,128)(2,1)}, u32[]{:S(2)}) copy-start(bf16[128,2048]{1,0:T(8,128)(2,1)} %get-tuple-element.32) | copy-start | bytes 1572868
  103.7 32.6 %collective-permute-start.4 = (bf16[128,2048]{1,0:T(8,128)(2,1)}, bf16[128,2048]{1,0:T(8,128)(2,1)}, u32[]{:S(2)}, u32[]{:S(2)}) collective-permute-start(bf16[128,2048]{1,0:T(8,128)(2,1)} %get-tuple-element.33), channel_id=1, source_target_pairs={{0,1},{1,0},{2,3},{3,2},{4,5},{5,4},{6,7},{7,6},{8,9},{9,8},{10,11... | collective-permute-start | bytes 1572872 | tf_op jit(solution)/shard_map/ppermute | solution.py:24
  103.8 2.2 %collective-permute-start.6 = (bf16[128,256]{1,0:T(8,128)(2,1)}, bf16[128,256]{1,0:T(8,128)(2,1)S(1)}, u32[]{:S(2)}, u32[]{:S(2)}) collective-permute-start(bf16[128,256]{1,0:T(8,128)(2,1)} %get-tuple-element.37), channel_id=1, source_target_pairs={{0,1},{1,0},{2,3},{3,2},{4,5},{5,4},{6,7},{7,6},{8,9},{9,8},{10,11... | collective-permute-start | bytes 196616 | tf_op jit(solution)/shard_map/ppermute | solution.py:24
  118.0 13.1 %all-to-all-start.3 = ((bf16[8,16,512]{2,1,0:T(8,128)(2,1)}), bf16[8,16,512]{2,1,0:T(8,128)(2,1)S(1)}, u32[]{:S(2)}, u32[]{:S(2)}) async-start(bf16[8,16,512]{2,1,0:T(8,128)(2,1)} %broadcast_in_dim.23), calls=%async_computation.3 | async-start | bytes 262144 | tf_op jit(solution)/shard_map/all_to_all | solution.py:29
  131.4 5.9 %collective-permute-start.7 = (bf16[8,8,640]{2,1,0:T(8,128)(2,1)S(1)}, bf16[8,8,640]{2,1,0:T(8,128)(2,1)S(1)}, u32[]{:S(2)}, u32[]{:S(2)}) collective-permute-start(bf16[8,8,640]{2,1,0:T(8,128)(2,1)S(1)} %fusion.4), channel_id=1, source_target_pairs={{0,1},{1,0},{2,3},{3,2},{4,5},{5,4},{6,7},{7,6},{8,9},{9,8},{10,11... | collective-permute-start | bytes 245768 | tf_op jit(solution)/shard_map/ppermute | solution.py:24
  138.0 10.7 %all-to-all-start.4 = ((bf16[8,8,640]{2,1,0:T(8,128)(2,1)}), bf16[8,8,640]{2,1,0:T(8,128)(2,1)S(1)}, u32[]{:S(2)}, u32[]{:S(2)}) async-start(bf16[8,8,640]{2,1,0:T(8,128)(2,1)} %fusion.2), calls=%async_computation.4 | async-start | bytes 163840 | tf_op jit(solution)/shard_map/all_to_all | solution.py:422

commit v2 on v1

--- a/solution.py
+++ b/solution.py
@@ -7,6 +7,7 @@
 from jax.experimental.pallas import tpu as pltpu
 from jax.sharding import Mesh
 from jax.sharding import PartitionSpec as P
+
 
 CAND = ("cand_0", "cand_1", "cand_2")
 GRP_CAND = ("grp", "cand_0", "cand_1", "cand_2")
@@ -22,6 +23,11 @@
 
 def swap(x):
     return lax.ppermute(x, PAIR, [(0, 1), (1, 0)])
+
+
+def shifted(x, by):
+    n = lax.axis_size(FAR)
+    return lax.ppermute(x, FAR, [(i, (i + by) % n) for i in range(n)])
 
 
 def from_everyone(shard, axis):
@@ -107,11 +113,13 @@
 
 
 def prompt_kernel(
-    meta, prompt, qs, gs, partial, ds_out, stats, prompt_grads, e_s, dp_s, dk_acc, dv_acc
+    meta, prompt, qs, gs, partial, ds_out, stats, prompt_grads,
+    e_0, dp_0, e_1, dp_1, dk_acc, dv_acc,
 ):
     total = prompt.shape[0]
     head_dim = qs.shape[-1]
-    rows = e_s.shape[1]
+    rows = e_0.shape[1]
+    buffers = ((e_0, dp_0), (e_1, dp_1))
     which = pl.program_id(1)
     length, seen = meta[2 * which], meta[2 * which + 1]
 
@@ -120,40 +128,56 @@
         dk_acc[...] = jnp.zeros(dk_acc.shape, jnp.float32)
         dv_acc[...] = jnp.zeros(dv_acc.shape, jnp.float32)
 
+    def first_pass(low, high, b, e_s, dp_s):
+        at = pl.ds(pl.multiple_of(b * rows, rows), rows)
+        q, go = qs[0, 0, at, :], gs[0, 0, at, :]
+        part = pl.multiple_of(b * 16, 16)
+        sums = partial[0, 0, pl.ds(part, 8), :]
+        dots = partial[0, 0, pl.ds(part + 8, 8), :]
+        for base in range(0, high, KEY_CHUNK):
+            chunk = slice(base, base + KEY_CHUNK)
+            e = exponent(prompt[chunk, :head_dim], q)
+            if base + KEY_CHUNK > low:
+                index = lax.broadcasted_iota(jnp.int32, (KEY_CHUNK, rows), 0)
+                e = jnp.where(index < seen - base, e, 0.0)
+            dp = contract_last(prompt[chunk, head_dim:], go)
+            e_s[chunk] = e
+            dp_s[chunk] = dp
+            sums += folded(e)
+            dots += folded(e * dp)
+        inverse = 1.0 / jnp.sum(sums, axis=0, keepdims=True)
+        delta = jnp.sum(dots, axis=0, keepdims=True) * inverse
+        stats[0, 0, pl.ds(part, 8), :] = jnp.broadcast_to(inverse, (8, rows))
+        stats[0, 0, pl.ds(part + 8, 8), :] = jnp.broadcast_to(delta, (8, rows))
+        return q, go, inverse, delta
+
+    def second_pass(high, b, e_s, dp_s, q, go, inverse, delta):
+        for base in range(0, high, KEY_CHUNK):
+            chunk = slice(base, base + KEY_CHUNK)
+            p = e_s[chunk] * inverse
+            ds = (p * (dp_s[chunk] - delta)).astype(jnp.bfloat16)
+            ds_out[0, 0, b, chunk, :] = ds
+            dv_acc[chunk] += jnp.dot(
+                p.astype(jnp.bfloat16), go, preferred_element_type=jnp.float32
+            )
+            dk_acc[chunk] += jnp.dot(ds, q, preferred_element_type=jnp.float32)
+
     def blocks(low, high):
-        def row_block(b, carry):
-            at = pl.ds(pl.multiple_of(b * rows, rows), rows)
-            q, go = qs[0, 0, at, :], gs[0, 0, at, :]
-            part = pl.multiple_of(b * 16, 16)
-            sums = partial[0, 0, pl.ds(part, 8), :]
-            dots = partial[0, 0, pl.ds(part + 8, 8), :]
-            for base in range(0, high, KEY_CHUNK):
-                chunk = slice(base, base + KEY_CHUNK)
-                e = exponent(prompt[chunk, :head_dim], q)
-                if base + KEY_CHUNK > low:
-                    index = lax.broadcasted_iota(jnp.int32, (KEY_CHUNK, rows), 0)
-                    e = jnp.where(index < seen - base, e, 0.0)
-                dp = contract_last(prompt[chunk, head_dim:], go)
-                e_s[chunk] = e
-                dp_s[chunk] = dp
-                sums += folded(e)
-                dots += folded(e * dp)
-            inverse = 1.0 / jnp.sum(sums, axis=0, keepdims=True)
-            delta = jnp.sum(dots, axis=0, keepdims=True) * inverse
-            stats[0, 0, pl.ds(part, 8), :] = jnp.broadcast_to(inverse, (8, rows))
-            stats[0, 0, pl.ds(part + 8, 8), :] = jnp.broadcast_to(delta, (8, rows))
-            for base in range(0, high, KEY_CHUNK):
-                chunk = slice(base, base + KEY_CHUNK)
-                p = e_s[chunk] * inverse
-                ds = (p * (dp_s[chunk] - delta)).astype(jnp.bfloat16)
-                ds_out[0, 0, b, chunk, :] = ds
-                dv_acc[chunk] += jnp.dot(
-                    p.astype(jnp.bfloat16), go, preferred_element_type=jnp.float32
-                )
-                dk_acc[chunk] += jnp.dot(ds, q, preferred_element_type=jnp.float32)
+        def run(some):
+            held = [first_pass(low, high, b, *buffers[i]) for i, b in enumerate(some)]
+            for i, b in enumerate(some):
+                second_pass(high, b, *buffers[i], *held[i])
+
+        def pair(i, carry):
+            run((2 * i, 2 * i + 1))
             return carry
 
-        lax.fori_loop(0, block_count(length), row_block, 0)
+        count = block_count(length)
+        lax.fori_loop(0, count // 2, pair, 0)
+
+        @pl.when(count % 2 == 1)
+        def _():
+            run((count - 1,))
 
     step = total // KEY_STEPS
     for n in range(1, KEY_STEPS + 1):
@@ -280,11 +304,15 @@
         compiler_params=limit(8),
         cost_estimate=cost(2, slots, 4 * 1024 * 1024),
     )(meta, own, own, own, own, other, other, other, other, q_gain, k_gain)
-    weight_pair, prompt, qs, gs, partial = lax.optimization_barrier(
-        (weight_pair, prompt, qs, gs, partial)
-    )
-    weight = from_everyone(weight_pair, FAR).reshape(-1, weight_pair.shape[1])
-    ds, stats, prompt_grads = pl.pallas_call(
+    above = [shifted(weight_pair, -k) for k in (1, 2, 3)]
+    above.append(shifted(above[-1], -1))
+    weight_pair, prompt, qs, gs, partial, *above = lax.optimization_barrier(
+        (weight_pair, prompt, qs, gs, partial, *above)
+    )
+    below = []
+    for k in (3, 2, 1):
+        below.append(shifted(weight_pair, k))
+    middle = pl.pallas_call(
         prompt_kernel,
         grid=(heads, 2),
         in_specs=[scalars, by_head(total, 2 * head_dim), by_unit(*stack), by_unit(*stack), by_unit(*stat)],
@@ -297,14 +325,17 @@
         scratch_shapes=[
             pltpu.VMEM((total, rows), high),
             pltpu.VMEM((total, rows), high),
+            pltpu.VMEM((total, rows), high),
+            pltpu.VMEM((total, rows), high),
             pltpu.VMEM((total, head_dim), high),
             pltpu.VMEM((total, head_dim), high),
         ],
         compiler_params=limit(57),
         cost_estimate=cost(4, total, 12 * 1024 * 1024),
-    )(meta, prompt, qs, gs, partial)
+    )
+    ds, stats, prompt_grads = middle(meta, prompt, qs, gs, partial)
     outs = [(slots, width), (slots, head_dim), (slots, head_dim)] * 2
-    grads = pl.pallas_call(
+    last = pl.pallas_call(
         after_kernel,
         grid=(heads,),
         in_specs=[scalars, q_side, k_side, v_side, q_side, k_side, v_side]
@@ -315,8 +346,11 @@
         scratch_shapes=[pltpu.VMEM((slots, head_dim), high), pltpu.VMEM((slots, head_dim), high)],
         compiler_params=limit(57),
         cost_estimate=cost(2, total, 14 * 1024 * 1024),
-    )(meta, own, own, own, other, other, other, prompt, qs, gs, ds, stats, q_gain, k_gain)
-    return (*grads, prompt_grads, weight)
+    )
+    grads = last(
+        meta, own, own, own, other, other, other, prompt, qs, gs, ds, stats, q_gain, k_gain
+    )
+    return (*grads, prompt_grads, [weight_pair, *above, *below])
 
 
 def on_device(
@@ -398,7 +432,10 @@
         heads, meta, own, other, prompt, weight_pair, q_gain, k_gain, width, head_dim
     )
 
-    sent, weight = lax.optimization_barrier((results[6], results[7]))
+    sent, *rows_from = lax.optimization_barrier((results[6], *results[7]))
+    ring = jnp.stack(rows_from + rows_from)
+    weight = lax.dynamic_slice_in_dim(ring, far - lax.axis_index(FAR), far, axis=0)
+    weight = weight.reshape(-1, 2 * narrow)
     sent = sent.reshape(far * near, count, 2 * narrow)
     parts = lax.all_to_all(sent, PLANE, 0, 0, tiled=True)
     total = jnp.sum(parts.astype(jnp.float32), axis=0).reshape(count, heads, 2, head_dim)

time: 151 us -> 179 us (1.19)
  waiting for transfers between devices: 42.7 us -> 62.1 us
  starting transfers between devices: 56.9 us -> 74.6 us
  Pallas kernels: 25 us -> 17.2 us
  other arithmetic: 11.5 us -> 8.85 us
    ppermute x0 -> x7, waiting for transfers between devices: none -> 21.7 us  [shifted(): return lax.ppermute(x, FAR, [(i, (i + by) % n) for i in range(n)])]
    ppermute x0 -> x7, starting transfers between devices: none -> 18.8 us  [shifted(): return lax.ppermute(x, FAR, [(i, (i + by) % n) for i in range(n)])]
    all_to_all x3 -> x2, waiting for transfers between devices: 25.8 us -> 7.87 us  [from_everyone(): return lax.all_to_all(copies, axis, split_axis=0, concat_axis=0, tiled=True)]
    all_to_all x1, waiting for transfers between devices: 9.76 us -> 25.6 us  [on_device(): parts = lax.all_to_all(sent, PLANE, 0, 0, tiled=True)]
    pallas_call x2, Pallas kernels: 21.4 us -> 14.8 us  [the longest x1 7.77 us: attend(): ds, stats, prompt_grads = middle(meta, prompt, qs, gs, partial)]
    all_to_all x1, starting transfers between devices: 6.69 us -> 12.4 us  [on_device(): parts = lax.all_to_all(sent, PLANE, 0, 0, tiled=True)]
    all_to_all x3 -> x2, starting transfers between devices: 18 us -> 12.3 us  [from_everyone(): return lax.all_to_all(copies, axis, split_axis=0, concat_axis=0, tiled=True)]
    select_n x5, other arithmetic: 3.62 us -> 1.8 us  [in_core_order(): return (jnp.where(flip, mine, theirs), jnp.where(flip, theirs, mine))]
  transfers between devices with their start and end apart: 13 -> 19, of which waited for: 8 -> 8; matrix products, arithmetic and copies ran while one was open for 10% -> 8% of each run, Pallas kernels for 17% -> 1%
where the time goes in v2:
time: 179 us; the launch traced here: 178 us
  starting transfers between devices  74.6 us (42%)
  waiting for transfers between devices  62.1 us (35%)
  Pallas kernels  17.2 us (10%)
  local copies, waits for them, and re-layouts  12.5 us (7%)
  other arithmetic  8.85 us (5%)
  between operations  2.61 us (1%)
    ppermute x8, starting transfers between devices, swap(): return lax.ppermute(x, PAIR, [(0, 1), (1, 0)])  27.5 us
    all_to_all x1, waiting for transfers between devices, on_device(): parts = lax.all_to_all(sent, PLANE, 0, 0, tiled=True)  25.6 us
    ppermute x7, waiting for transfers between devices, shifted(): return lax.ppermute(x, FAR, [(i, (i + by) % n) for i in range(n)])  21.7 us
    ppermute x7, starting transfers between devices, shifted(): return lax.ppermute(x, FAR, [(i, (i + by) % n) for i in range(n)])  18.8 us
    all_to_all x1, starting transfers between devices, on_device(): parts = lax.all_to_all(sent, PLANE, 0, 0, tiled=True)  12.4 us
    all_to_all x2, starting transfers between devices, from_everyone(): return lax.all_to_all(copies, axis, split_axis=0, concat_axis=0, tiled=True)  12.3 us
    all_to_all x2, waiting for transfers between devices, from_everyone(): return lax.all_to_all(copies, axis, split_axis=0, concat_axis=0, tiled=True)  7.87 us
    pallas_call x1, Pallas kernels, attend(): ds, stats, prompt_grads = middle(meta, prompt, qs, gs, partial)  7.77 us
  transfers between devices with their start and end apart: 19, of which 8 were waited for; matrix products, arithmetic and copies ran while one was open for 8% of the time, Pallas kernels for 1%

profile of v2, /device:TPU:513, one launch (start us, length us, event | category | flops | bytes accessed | tf_op | source)
XLA Modules:
  0.0 178.3 jit_solution(2790285015954554259)
XLA Ops:
  0.6 0.7 constant_dynamic-slice_fusion.3
  1.4 20.4 %collective-permute-start.3 = (bf16[8,512]{1,0:T(8,128)(2,1)S(1)}, bf16[8,512]{1,0:T(8,128)(2,1)S(1)}, u32[]{:S(2)}, u32[]{:S(2)}) collective-permute-start(bf16[8,512]{1,0:T(8,128)(2,1)S(1)} %pad_maximum_fusion.8), channel_id=1, source_target_pairs={{0,1},{1,0},{2,3},{3,2},{4,5},{5,4},{6,7},{7,6},{8,9},{9,8},{10,11... | collective-permute-start | bytes 24584 | tf_op jit(solution)/shard_map/ppermute | solution.py:25
  21.8 0.7 broadcast_bitcast_fusion
  22.5 1.7 constant_dynamic-slice_fusion.9
  24.3 0.1 multiply_reduce_fusion.1
  24.4 0.6 multiply_multiply_fusion
  25.0 0.1 mul.123
  25.1 1.1 broadcast_in_dim.16
  26.2 6.5 %all-to-all-start = ((bf16[64,16,512]{2,1,0:T(8,128)(2,1)}), bf16[64,16,512]{2,1,0:T(8,128)(2,1)S(1)}, u32[]{:S(2)}, u32[]{:S(2)}) async-start(bf16[64,16,512]{2,1,0:T(8,128)(2,1)} %broadcast_in_dim.16), calls=%async_computation | async-start | bytes 2097152 | tf_op jit(solution)/shard_map/all_to_all | solution.py:35
  32.7 1.1 pad_maximum_fusion.1
  33.9 0.0 collective-permute-start.1
  33.9 0.9 reshape.83
  34.8 0.1 constant_dynamic-slice_fusion.6
  35.0 0.6 reshape.85
  35.6 0.5 collective-permute-start.2
  37.4 0.1 pad_add_fusion
  37.5 0.1 collective-permute-start
  37.7 0.0 copy-start.4
  37.7 3.9 %collective-permute-start.6 = (bf16[80,512]{1,0:T(8,128)(2,1)S(1)}, bf16[80,512]{1,0:T(8,128)(2,1)S(1)}, u32[]{:S(2)}, u32[]{:S(2)}) collective-permute-start(bf16[80,512]{1,0:T(8,128)(2,1)S(1)} %pad_maximum_fusion.5), channel_id=1, source_target_pairs={{0,80},{16,96},{32,112},{48,0},{64,16},{80,32},{96,48},{112,64},{1... | collective-permute-start | bytes 245768 | tf_op jit(solution)/shard_map/ppermute | solution.py:30
  41.7 0.1 pad_maximum_fusion.q_own.g_own.k_own.v_own
  41.7 1.1 collective-permute-start.4
  42.9 15.3 %collective-permute-done.6 = bf16[80,512]{1,0:T(8,128)(2,1)S(1)} collective-permute-done((bf16[80,512]{1,0:T(8,128)(2,1)S(1)}, bf16[80,512]{1,0:T(8,128)(2,1)S(1)}, u32[]{:S(2)}, u32[]{:S(2)}) %collective-permute-start.6) | collective-permute-done | bytes 81952 | tf_op jit(solution)/shard_map/ppermute | solution.py:30
  58.2 3.5 %collective-permute-start.7 = (bf16[80,512]{1,0:T(8,128)(2,1)S(1)}, bf16[80,512]{1,0:T(8,128)(2,1)S(1)}, u32[]{:S(2)}, u32[]{:S(2)}) collective-permute-start(bf16[80,512]{1,0:T(8,128)(2,1)S(1)} %collective-permute-done.6), channel_id=1, source_target_pairs={{0,112},{16,0},{32,16},{48,32},{64,48},{80,64},{96,80},{112,96},{1... | collective-permute-start | bytes 245768 | tf_op jit(solution)/shard_map/ppermute | solution.py:30
  61.7 0.1 pad_add_fusion.1.meta
  61.8 2.5 %shard_map.138 = (bf16[2,2,1024,128]{3,2,1,0:T(8,128)(2,1)S(1)}, bf16[2,2,1024,128]{3,2,1,0:T(8,128)(2,1)S(1)}, f32[2,2,64,256]{3,2,1,0:T(8,128)S(1)}) custom-call(s32[4]{0:T(128)S(1)} %pad_add_fusion.1.meta, bf16[128,4608]{1,0:T(8,128)(2,1)S(1)} %pad_maximum_fusion.q_own.g_own.k_own.v_own, bf16[128,4608]{1,0:T(8,128)(2,1)S(1)} %pad_maximum_fusion.q_own.g_own.k_own.v_own, ...), custom_call_target="tpu_custom_call" | custom-call | flops 268435456 | bytes 4194304 | tf_op jit(solution)/shard_map/pallas_call | solution.py:298
  64.3 1.0 copy-done.2
  65.4 1.0 copy-done.3
  66.3 0.7 copy-done.8
  67.1 1.0 copy-done.9
  68.1 7.8 %shard_map.139 = (bf16[2,2,4,1024,256]{4,3,2,1,0:T(8,128)(2,1)}, f32[2,2,64,256]{3,2,1,0:T(8,128)}, bf16[1024,512]{1,0:T(8,128)(2,1)}) custom-call(s32[4]{0:T(128)} %copy-done.6, bf16[1024,512]{1,0:T(8,128)(2,1)} %bitcast.68, bf16[2,2,1024,128]{3,2,1,0:T(8,128)(2,1)} %copy-done.2, bf16[2,2,1024,128]{3,2,1,0:T(8,128)(2,1)} %copy-done.3, ...), custom_call_target="tpu_custom_call" | custom-call | flops 4294967296 | bytes 12582912 | tf_op jit(solution)/shard_map/pallas_call | solution.py:336
  75.9 7.0 %shard_map.140 = (bf16[128,2048]{1,0:T(8,128)(2,1)}, bf16[128,256]{1,0:T(8,128)(2,1)}, bf16[128,256]{1,0:T(8,128)(2,1)}, bf16[128,2048]{1,0:T(8,128)(2,1)}, bf16...) custom-call(s32[4]{0:T(128)} %copy-done.6, bf16[128,4608]{1,0:T(8,128)(2,1)} %copy-done, bf16[128,4608]{1,0:T(8,128)(2,1)} %copy-done, ...), custom_call_target="tpu_custom_call" | custom-call | flops 2147483648 | bytes 14680064 | tf_op jit(solution)/shard_map/pallas_call | solution.py:350
  82.9 2.2 %collective-permute-start.9 = (bf16[128,256]{1,0:T(8,128)(2,1)}, bf16[128,256]{1,0:T(8,128)(2,1)S(1)}, u32[]{:S(2)}, u32[]{:S(2)}) collective-permute-start(bf16[128,256]{1,0:T(8,128)(2,1)} %get-tuple-element.46), channel_id=1, source_target_pairs={{0,1},{1,0},{2,3},{3,2},{4,5},{5,4},{6,7},{7,6},{8,9},{9,8},{10,11... | collective-permute-start | bytes 196616 | tf_op jit(solution)/shard_map/ppermute | solution.py:25
  85.1 0.6 reshape.90
  85.7 9.5 %collective-permute-start.11 = (bf16[80,512]{1,0:T(8,128)(2,1)S(1)}, bf16[80,512]{1,0:T(8,128)(2,1)S(1)}, u32[]{:S(2)}, u32[]{:S(2)}) collective-permute-start(bf16[80,512]{1,0:T(8,128)(2,1)S(1)} %pad_maximum_fusion.5), channel_id=1, source_target_pairs={{0,48},{16,64},{32,80},{48,96},{64,112},{80,0},{96,16},{112,32},{1... | collective-permute-start | bytes 245768 | tf_op jit(solution)/shard_map/ppermute | solution.py:30
  95.2 0.7 collective-permute-start.13
  95.9 0.3 collective-permute-start.8
  96.2 0.2 collective-permute-start.10
  96.4 0.9 broadcast_select_fusion.5
  97.3 0.7 pad_maximum_fusion.3
  98.0 0.2 collective-permute-done.10
  98.1 0.9 broadcast_select_fusion.3
  99.0 0.7 pad_maximum_fusion.4
  99.7 5.1 %collective-permute-done.12 = bf16[80,512]{1,0:T(8,128)(2,1)S(1)} collective-permute-done((bf16[80,512]{1,0:T(8,128)(2,1)S(1)}, bf16[80,512]{1,0:T(8,128)(2,1)S(1)}, u32[]{:S(2)}, u32[]{:S(2)}) %collective-permute-start.12) | collective-permute-done | bytes 81952 | tf_op jit(solution)/shard_map/ppermute | solution.py:30
  104.8 1.2 collective-permute-done.13
  106.0 12.4 %all-to-all-start.1 = ((bf16[64,16,512]{2,1,0:T(8,128)(2,1)}), bf16[64,16,512]{2,1,0:T(8,128)(2,1)S(1)}, u32[]{:S(2)}, u32[]{:S(2)}) async-start(bf16[64,16,512]{2,1,0:T(8,128)(2,1)} %bitcast.8), calls=%async_computation.1 | async-start | bytes 2097152 | tf_op jit(solution)/shard_map/all_to_all | solution.py:440
  118.7 25.6 %all-to-all-done.1 = bf16[64,16,512]{2,1,0:T(8,128)(2,1)S(1)} async-done(((bf16[64,16,512]{2,1,0:T(8,128)(2,1)}), bf16[64,16,512]{2,1,0:T(8,128)(2,1)S(1)}, u32[]{:S(2)}, u32[]{:S(2)}) %all-to-all-start.1) | async-done | bytes 1048608 | tf_op jit(solution)/shard_map/all_to_all | solution.py:440
  144.3 0.2 convert_reduce_fusion
  144.6 0.8 multiply_reduce_fusion
  145.4 0.9 subtract_convert_fusion
  146.4 0.7 broadcast_in_dim.19
  147.0 5.8 %all-to-all-start.2 = ((bf16[8,16,512]{2,1,0:T(8,128)(2,1)}), bf16[8,16,512]{2,1,0:T(8,128)(2,1)S(1)}, u32[]{:S(2)}, u32[]{:S(2)}) async-start(bf16[8,16,512]{2,1,0:T(8,128)(2,1)} %broadcast_in_dim.19), calls=%async_computation.2 | async-start | bytes 262144 | tf_op jit(solution)/shard_map/all_to_all | solution.py:35
  152.9 0.1 constant_dynamic-slice_fusion
  152.9 7.9 %all-to-all-done.2 = bf16[8,16,512]{2,1,0:T(8,128)(2,1)S(1)} async-done(((bf16[8,16,512]{2,1,0:T(8,128)(2,1)}), bf16[8,16,512]{2,1,0:T(8,128)(2,1)S(1)}, u32[]{:S(2)}, u32[]{:S(2)}) %all-to-all-start.2) | async-done | bytes 131104 | tf_op jit(solution)/shard_map/all_to_all | solution.py:35
  160.8 0.4 fusion.1
  161.2 3.8 %collective-permute-start.14 = (bf16[8,8,640]{2,1,0:T(8,128)(2,1)S(1)}, bf16[8,8,640]{2,1,0:T(8,128)(2,1)S(1)}, u32[]{:S(2)}, u32[]{:S(2)}) collective-permute-start(bf16[8,8,640]{2,1,0:T(8,128)(2,1)S(1)} %fusion.3), channel_id=1, source_target_pairs={{0,1},{1,0},{2,3},{3,2},{4,5},{5,4},{6,7},{7,6},{8,9},{9,8},{10,11... | collective-permute-start | bytes 245768 | tf_op jit(solution)/shard_map/ppermute | solution.py:25
  165.0 0.1 broadcast_select_fusion.1
  165.1 0.8 collective-permute-done.14
  165.9 0.7 fusion
  166.6 3.6 %all-to-all-start.3 = ((bf16[8,8,640]{2,1,0:T(8,128)(2,1)}), bf16[8,8,640]{2,1,0:T(8,128)(2,1)S(1)}, u32[]{:S(2)}, u32[]{:S(2)}) async-start(bf16[8,8,640]{2,1,0:T(8,128)(2,1)} %fusion), calls=%async_computation.3 | async-start | bytes 163840 | tf_op jit(solution)/shard_map/all_to_all | solution.py:459
  170.2 1.0 pad_maximum_fusion.2
  171.2 6.0 %all-to-all-done.3 = bf16[8,8,640]{2,1,0:T(8,128)(2,1)S(1)} async-done(((bf16[8,8,640]{2,1,0:T(8,128)(2,1)}), bf16[8,8,640]{2,1,0:T(8,128)(2,1)S(1)}, u32[]{:S(2)}, u32[]{:S(2)}) %all-to-all-start.3) | async-done | bytes 81952 | tf_op jit(solution)/shard_map/all_to_all | solution.py:459
  177.2 0.2 reshape.92
  177.3 0.1 copy.21
  177.4 0.8 reshape.93
  (92 shorter events, 0.6 us)
Async XLA Ops:
  1.4 22.8 %collective-permute-start.3 = (bf16[8,512]{1,0:T(8,128)(2,1)S(1)}, bf16[8,512]{1,0:T(8,128)(2,1)S(1)}, u32[]{:S(2)}, u32[]{:S(2)}) collective-permute-start(bf16[8,512]{1,0:T(8,128)(2,1)S(1)} %pad_maximum_fusion.8), channel_id=1, source_target_pairs={{0,1},{1,0},{2,3},{3,2},{4,5},{5,4},{6,7},{7,6},{8,9},{9,8},{10,11... | collective-permute-start | bytes 24584 | tf_op jit(solution)/shard_map/ppermute | solution.py:25
  22.5 1.7 copy-start.20
  22.5 1.7 copy-start.21
  24.3 1.9 %copy-start.19 = (f32[16,2,128]{2,1,0:T(2,128)}, f32[16,2,128]{2,1,0:T(2,128)S(1)}, u32[]{:S(2)}) copy-start(f32[16,2,128]{2,1,0:T(2,128)S(1)} %reshape.86) | copy-start | bytes 49156
  25.0 1.2 copy-start.22
  26.2 40.9 %all-to-all-start = ((bf16[64,16,512]{2,1,0:T(8,128)(2,1)}), bf16[64,16,512]{2,1,0:T(8,128)(2,1)S(1)}, u32[]{:S(2)}, u32[]{:S(2)}) async-start(bf16[64,16,512]{2,1,0:T(8,128)(2,1)} %broadcast_in_dim.16), calls=%async_computation | async-start | bytes 2097152 | tf_op jit(solution)/shard_map/all_to_all | solution.py:35
  33.9 27.9 %collective-permute-start.1 = (bf16[128,4608]{1,0:T(8,128)(2,1)}, bf16[128,4608]{1,0:T(8,128)(2,1)S(1)}, u32[]{:S(2)}, u32[]{:S(2)}) collective-permute-start(bf16[128,4608]{1,0:T(8,128)(2,1)} %pad_maximum_fusion.1), channel_id=1, source_target_pairs={{0,1},{1,0},{2,3},{3,2},{4,5},{5,4},{6,7},{7,6},{8,9},{9,8},{10,11... | collective-permute-start | bytes 3538952 | tf_op jit(solution)/shard_map/ppermute | solution.py:25
  35.6 2.0 %collective-permute-start.2 = (bf16[40,512]{1,0:T(8,128)(2,1)}, bf16[40,512]{1,0:T(8,128)(2,1)S(1)}, u32[]{:S(2)}, u32[]{:S(2)}) collective-permute-start(bf16[40,512]{1,0:T(8,128)(2,1)} %reshape.85), channel_id=1, source_target_pairs={{0,1},{1,0},{2,3},{3,2},{4,5},{5,4},{6,7},{7,6},{8,9},{9,8},{10,11... | collective-permute-start | bytes 122888 | tf_op jit(solution)/shard_map/ppermute | solution.py:25
  37.5 24.2 %collective-permute-start = (s32[2]{0:T(128)S(1)}, s32[2]{0:T(128)S(1)}, u32[]{:S(2)}, u32[]{:S(2)}) collective-permute-start(s32[2]{0:T(128)S(1)} %pad_add_fusion), channel_id=1, source_target_pairs={{0,1},{1,0},{2,3},{3,2},{4,5},{5,4},{6,7},{7,6},{8,9},{9,8},{10,11... | collective-permute-start | bytes 32 | tf_op jit(solution)/shard_map/ppermute | solution.py:25
  37.7 24.1 %copy-start.4 = (f32[128]{0:T(128)S(1)}, f32[128]{0:T(128)}, u32[]{:S(2)}) copy-start(f32[128]{0:T(128)} %param.20) | copy-start | bytes 1540
  37.7 24.1 %copy-start.7 = (f32[128]{0:T(128)S(1)}, f32[128]{0:T(128)}, u32[]{:S(2)}) copy-start(f32[128]{0:T(128)} %param.19) | copy-start | bytes 1540
  37.7 20.5 %collective-permute-start.6 = (bf16[80,512]{1,0:T(8,128)(2,1)S(1)}, bf16[80,512]{1,0:T(8,128)(2,1)S(1)}, u32[]{:S(2)}, u32[]{:S(2)}) collective-permute-start(bf16[80,512]{1,0:T(8,128)(2,1)S(1)} %pad_maximum_fusion.5), channel_id=1, source_target_pairs={{0,80},{16,96},{32,112},{48,0},{64,16},{80,32},{96,48},{112,64},{1... | collective-permute-start | bytes 245768 | tf_op jit(solution)/shard_map/ppermute | solution.py:30
  41.7 22.6 %copy-start = (bf16[128,4608]{1,0:T(8,128)(2,1)}, bf16[128,4608]{1,0:T(8,128)(2,1)S(1)}, u32[]{:S(2)}) copy-start(bf16[128,4608]{1,0:T(8,128)(2,1)S(1)} %pad_maximum_fusion.q_own.g_own.k_own.v_own) | copy-start | bytes 3538948
  41.7 25.3 %collective-permute-start.4 = (bf16[80,512]{1,0:T(8,128)(2,1)S(1)}, bf16[80,512]{1,0:T(8,128)(2,1)S(1)}, u32[]{:S(2)}, u32[]{:S(2)}) collective-permute-start(bf16[80,512]{1,0:T(8,128)(2,1)S(1)} %pad_maximum_fusion.5), channel_id=1, source_target_pairs={{0,112},{16,0},{32,16},{48,32},{64,48},{80,64},{96,80},{112,96},{1... | collective-permute-start | bytes 245768 | tf_op jit(solution)/shard_map/ppermute | solution.py:30
  42.9 24.2 %collective-permute-start.5 = (bf16[80,512]{1,0:T(8,128)(2,1)S(1)}, bf16[80,512]{1,0:T(8,128)(2,1)S(1)}, u32[]{:S(2)}, u32[]{:S(2)}) collective-permute-start(bf16[80,512]{1,0:T(8,128)(2,1)S(1)} %pad_maximum_fusion.5), channel_id=1, source_target_pairs={{0,96},{16,112},{32,0},{48,16},{64,32},{80,48},{96,64},{112,80},{1... | collective-permute-start | bytes 245768 | tf_op jit(solution)/shard_map/ppermute | solution.py:30
  58.2 6.1 %copy-start.11 = (bf16[80,512]{1,0:T(8,128)(2,1)}, bf16[80,512]{1,0:T(8,128)(2,1)S(1)}, u32[]{:S(2)}) copy-start(bf16[80,512]{1,0:T(8,128)(2,1)S(1)} %collective-permute-done.6) | copy-start | bytes 245764
  58.2 8.9 %collective-permute-start.7 = (bf16[80,512]{1,0:T(8,128)(2,1)S(1)}, bf16[80,512]{1,0:T(8,128)(2,1)S(1)}, u32[]{:S(2)}, u32[]{:S(2)}) collective-permute-start(bf16[80,512]{1,0:T(8,128)(2,1)S(1)} %collective-permute-done.6), channel_id=1, source_target_pairs={{0,112},{16,0},{32,16},{48,32},{64,48},{80,64},{96,80},{112,96},{1... | collective-permute-start | bytes 245768 | tf_op jit(solution)/shard_map/ppermute | solution.py:30
  61.8 2.5 %copy-start.6 = (s32[4]{0:T(128)}, s32[4]{0:T(128)S(1)}, u32[]{:S(2)}) copy-start(s32[4]{0:T(128)S(1)} %pad_add_fusion.1.meta) | copy-start | bytes 52
  61.8 2.5 %copy-start.1 = (bf16[128,4608]{1,0:T(8,128)(2,1)}, bf16[128,4608]{1,0:T(8,128)(2,1)S(1)}, u32[]{:S(2)}) copy-start(bf16[128,4608]{1,0:T(8,128)(2,1)S(1)} %collective-permute-done.1.q_other.g_other.k_other.v_other) | copy-start | bytes 3538948
  64.3 1.0 copy-start.2
  65.4 1.0 copy-start.3
  66.3 0.7 copy-start.8
  67.1 8.8 %copy-start.13 = (bf16[80,512]{1,0:T(8,128)(2,1)}, bf16[80,512]{1,0:T(8,128)(2,1)S(1)}, u32[]{:S(2)}) copy-start(bf16[80,512]{1,0:T(8,128)(2,1)S(1)} %collective-permute-done.4) | copy-start | bytes 245764
  67.1 8.8 %copy-start.15 = (bf16[80,512]{1,0:T(8,128)(2,1)}, bf16[80,512]{1,0:T(8,128)(2,1)S(1)}, u32[]{:S(2)}) copy-start(bf16[80,512]{1,0:T(8,128)(2,1)S(1)} %collective-permute-done.5) | copy-start | bytes 245764
  67.1 8.8 %copy-start.17 = (bf16[80,512]{1,0:T(8,128)(2,1)}, bf16[80,512]{1,0:T(8,128)(2,1)S(1)}, u32[]{:S(2)}) copy-start(bf16[80,512]{1,0:T(8,128)(2,1)S(1)} %collective-permute-done.7) | copy-start | bytes 245764
  67.1 1.0 copy-start.9
  82.9 13.3 %collective-permute-start.9 = (bf16[128,256]{1,0:T(8,128)(2,1)}, bf16[128,256]{1,0:T(8,128)(2,1)S(1)}, u32[]{:S(2)}, u32[]{:S(2)}) collective-permute-start(bf16[128,256]{1,0:T(8,128)(2,1)} %get-tuple-element.46), channel_id=1, source_target_pairs={{0,1},{1,0},{2,3},{3,2},{4,5},{5,4},{6,7},{7,6},{8,9},{9,8},{10,11... | collective-permute-start | bytes 196616 | tf_op jit(solution)/shard_map/ppermute | solution.py:25
  85.7 14.0 %collective-permute-start.11 = (bf16[80,512]{1,0:T(8,128)(2,1)S(1)}, bf16[80,512]{1,0:T(8,128)(2,1)S(1)}, u32[]{:S(2)}, u32[]{:S(2)}) collective-permute-start(bf16[80,512]{1,0:T(8,128)(2,1)S(1)} %pad_maximum_fusion.5), channel_id=1, source_target_pairs={{0,48},{16,64},{32,80},{48,96},{64,112},{80,0},{96,16},{112,32},{1... | collective-permute-start | bytes 245768 | tf_op jit(solution)/shard_map/ppermute | solution.py:30
  95.2 9.5 %collective-permute-start.12 = (bf16[80,512]{1,0:T(8,128)(2,1)S(1)}, bf16[80,512]{1,0:T(8,128)(2,1)S(1)}, u32[]{:S(2)}, u32[]{:S(2)}) collective-permute-start(bf16[80,512]{1,0:T(8,128)(2,1)S(1)} %pad_maximum_fusion.5), channel_id=1, source_target_pairs={{0,32},{16,48},{32,64},{48,80},{64,96},{80,112},{96,0},{112,16},{1... | collective-permute-start | bytes 245768 | tf_op jit(solution)/shard_map/ppermute | solution.py:30
  95.2 10.8 %collective-permute-start.13 = (bf16[80,512]{1,0:T(8,128)(2,1)S(1)}, bf16[80,512]{1,0:T(8,128)(2,1)S(1)}, u32[]{:S(2)}, u32[]{:S(2)}) collective-permute-start(bf16[80,512]{1,0:T(8,128)(2,1)S(1)} %pad_maximum_fusion.5), channel_id=1, source_target_pairs={{0,16},{16,32},{32,48},{48,64},{64,80},{80,96},{96,112},{112,0},{1... | collective-permute-start | bytes 245768 | tf_op jit(solution)/shard_map/ppermute | solution.py:30
  95.9 69.1 %collective-permute-start.8 = (bf16[128,2048]{1,0:T(8,128)(2,1)}, bf16[128,2048]{1,0:T(8,128)(2,1)S(1)}, u32[]{:S(2)}, u32[]{:S(2)}) collective-permute-start(bf16[128,2048]{1,0:T(8,128)(2,1)} %get-tuple-element.44), channel_id=1, source_target_pairs={{0,1},{1,0},{2,3},{3,2},{4,5},{5,4},{6,7},{7,6},{8,9},{9,8},{10,11... | collective-permute-start | bytes 1572872 | tf_op jit(solution)/shard_map/ppermute | solution.py:25
  96.2 1.9 %collective-permute-start.10 = (bf16[128,256]{1,0:T(8,128)(2,1)}, bf16[128,256]{1,0:T(8,128)(2,1)S(1)}, u32[]{:S(2)}, u32[]{:S(2)}) collective-permute-start(bf16[128,256]{1,0:T(8,128)(2,1)} %get-tuple-element.48), channel_id=1, source_target_pairs={{0,1},{1,0},{2,3},{3,2},{4,5},{5,4},{6,7},{7,6},{8,9},{9,8},{10,11... | collective-permute-start | bytes 196616 | tf_op jit(solution)/shard_map/ppermute | solution.py:25
  99.0 19.5 %copy-start.14 = (bf16[80,512]{1,0:T(8,128)(2,1)S(1)}, bf16[80,512]{1,0:T(8,128)(2,1)}, u32[]{:S(2)}) copy-start(bf16[80,512]{1,0:T(8,128)(2,1)} %copy-done.13) | copy-start | bytes 245764
  99.0 19.5 %copy-start.16 = (bf16[80,512]{1,0:T(8,128)(2,1)S(1)}, bf16[80,512]{1,0:T(8,128)(2,1)}, u32[]{:S(2)}) copy-start(bf16[80,512]{1,0:T(8,128)(2,1)} %copy-done.15) | copy-start | bytes 245764
  99.7 18.8 %copy-start.12 = (bf16[80,512]{1,0:T(8,128)(2,1)S(1)}, bf16[80,512]{1,0:T(8,128)(2,1)}, u32[]{:S(2)}) copy-start(bf16[80,512]{1,0:T(8,128)(2,1)} %copy-done.11) | copy-start | bytes 245764
  106.0 12.5 %copy-start.18 = (bf16[80,512]{1,0:T(8,128)(2,1)S(1)}, bf16[80,512]{1,0:T(8,128)(2,1)}, u32[]{:S(2)}) copy-start(bf16[80,512]{1,0:T(8,128)(2,1)} %copy-done.17) | copy-start | bytes 245764
  106.0 38.3 %all-to-all-start.1 = ((bf16[64,16,512]{2,1,0:T(8,128)(2,1)}), bf16[64,16,512]{2,1,0:T(8,128)(2,1)S(1)}, u32[]{:S(2)}, u32[]{:S(2)}) async-start(bf16[64,16,512]{2,1,0:T(8,128)(2,1)} %bitcast.8), calls=%async_computation.1 | async-start | bytes 2097152 | tf_op jit(solution)/shard_map/all_to_all | solution.py:440
  118.6 26.0 %copy-start.5 = (f32[128]{0:T(128)S(1)}, f32[128]{0:T(128)}, u32[]{:S(2)}) copy-start(f32[128]{0:T(128)} %param.20) | copy-start | bytes 1540
  147.0 13.8 %all-to-all-start.2 = ((bf16[8,16,512]{2,1,0:T(8,128)(2,1)}), bf16[8,16,512]{2,1,0:T(8,128)(2,1)S(1)}, u32[]{:S(2)}, u32[]{:S(2)}) async-start(bf16[8,16,512]{2,1,0:T(8,128)(2,1)} %broadcast_in_dim.19), calls=%async_computation.2 | async-start | bytes 262144 | tf_op jit(solution)/shard_map/all_to_all | solution.py:35
  152.9 12.1 %copy-start.10 = (bf16[128,2048]{1,0:T(8,128)(2,1)S(1)}, bf16[128,2048]{1,0:T(8,128)(2,1)}, u32[]{:S(2)}) copy-start(bf16[128,2048]{1,0:T(8,128)(2,1)} %get-tuple-element.43) | copy-start | bytes 1572868
  161.2 4.7 %collective-permute-start.14 = (bf16[8,8,640]{2,1,0:T(8,128)(2,1)S(1)}, bf16[8,8,640]{2,1,0:T(8,128)(2,1)S(1)}, u32[]{:S(2)}, u32[]{:S(2)}) collective-permute-start(bf16[8,8,640]{2,1,0:T(8,128)(2,1)S(1)} %fusion.3), channel_id=1, source_target_pairs={{0,1},{1,0},{2,3},{3,2},{4,5},{5,4},{6,7},{7,6},{8,9},{9,8},{10,11... | collective-permute-start | bytes 245768 | tf_op jit(solution)/shard_map/ppermute | solution.py:25
  166.6 10.6 %all-to-all-start.3 = ((bf16[8,8,640]{2,1,0:T(8,128)(2,1)}), bf16[8,8,640]{2,1,0:T(8,128)(2,1)S(1)}, u32[]{:S(2)}, u32[]{:S(2)}) async-start(bf16[8,8,640]{2,1,0:T(8,128)(2,1)} %fusion), calls=%async_computation.3 | async-start | bytes 163840 | tf_op jit(solution)/shard_map/all_to_all | solution.py:459

commit v3 on v2

--- a/solution.py
+++ b/solution.py
@@ -13,6 +13,7 @@
 GRP_CAND = ("grp", "cand_0", "cand_1", "cand_2")
 PLANE = ("cand_0", "cand_1")
 FAR, NEAR, PAIR = CAND
+NEARBY = (3, 2, 1)
 ROW_SLOTS = 32
 KEY_CHUNK = 128
 KEY_STEPS = 4
@@ -254,6 +255,12 @@
         dv_ref[...] = dv_acc[...].astype(jnp.bfloat16)
 
 
+def place_kernel(place, *refs):
+    blocks, out = refs[:-1], refs[-1]
+    for j, block in enumerate(blocks):
+        out[lax.rem(place[0] + j, len(blocks))] = block[...]
+
+
 def attend(heads, meta, own, other, prompt, weight_pair, q_gain, k_gain, width, head_dim):
     slots, total = own.shape[0], prompt.shape[0]
     group = width // head_dim
@@ -304,14 +311,13 @@
         compiler_params=limit(8),
         cost_estimate=cost(2, slots, 4 * 1024 * 1024),
     )(meta, own, own, own, own, other, other, other, other, q_gain, k_gain)
-    above = [shifted(weight_pair, -k) for k in (1, 2, 3)]
-    above.append(shifted(above[-1], -1))
-    weight_pair, prompt, qs, gs, partial, *above = lax.optimization_barrier(
-        (weight_pair, prompt, qs, gs, partial, *above)
-    )
-    below = []
-    for k in (3, 2, 1):
+    weight_pair, prompt, qs, gs, partial = lax.optimization_barrier(
+        (weight_pair, prompt, qs, gs, partial)
+    )
+    above, below = [], []
+    for k in NEARBY:
         below.append(shifted(weight_pair, k))
+        above.append(shifted(weight_pair, -k))
     middle = pl.pallas_call(
         prompt_kernel,
         grid=(heads, 2),
@@ -432,9 +438,22 @@
         heads, meta, own, other, prompt, weight_pair, q_gain, k_gain, width, head_dim
     )
 
-    sent, *rows_from = lax.optimization_barrier((results[6], *results[7]))
-    ring = jnp.stack(rows_from + rows_from)
-    weight = lax.dynamic_slice_in_dim(ring, far - lax.axis_index(FAR), far, axis=0)
+    sent, here, *arrived = lax.optimization_barrier((results[6], *results[7]))
+    above, below = dict(zip(NEARBY, arrived[: len(NEARBY)])), dict(zip(NEARBY, arrived[len(NEARBY) :]))
+    across = shifted(above[3], -1)
+    ring = [here, above[1], above[2], above[3], across, below[3], below[2], below[1]]
+    place = jnp.reshape(lax.axis_index(FAR), (1,))
+    weight = pl.pallas_call(
+        place_kernel,
+        in_specs=[pl.BlockSpec(memory_space=pltpu.SMEM)]
+        + [pl.BlockSpec(memory_space=pltpu.VMEM)] * far,
+        out_specs=pl.BlockSpec(memory_space=pltpu.VMEM),
+        out_shape=jax.ShapeDtypeStruct((far, *here.shape), here.dtype),
+        compiler_params=pltpu.CompilerParams(vmem_limit_bytes=8 * 1024 * 1024),
+        cost_estimate=pl.CostEstimate(
+            flops=10**8, bytes_accessed=2 * far * here.size * 2, transcendentals=0
+        ),
+    )(place.astype(jnp.int32), *ring)
     weight = weight.reshape(-1, 2 * narrow)
     sent = sent.reshape(far * near, count, 2 * narrow)
     parts = lax.all_to_all(sent, PLANE, 0, 0, tiled=True)

time: 179 us -> 147 us (0.82)
  waiting for transfers between devices: 62.1 us -> 38.6 us
  starting transfers between devices: 74.6 us -> 67.6 us
  local copies, waits for them, and re-layouts: 12.5 us -> 10 us
    ppermute x7, waiting for transfers between devices: 21.7 us -> 5 us  [shifted(): return lax.ppermute(x, FAR, [(i, (i + by) % n) for i in range(n)])]
    all_to_all x1, waiting for transfers between devices: 25.6 us -> 9.11 us  [on_device(): parts = lax.all_to_all(sent, PLANE, 0, 0, tiled=True)]
    all_to_all x2, waiting for transfers between devices: 7.87 us -> 16.7 us  [from_everyone(): return lax.all_to_all(copies, axis, split_axis=0, concat_axis=0, tiled=True)]
    ppermute x7, starting transfers between devices: 18.8 us -> 11.4 us  [shifted(): return lax.ppermute(x, FAR, [(i, (i + by) % n) for i in range(n)])]
    ppermute x8, starting transfers between devices: 27.5 us -> 31.3 us  [swap(): return lax.ppermute(x, PAIR, [(0, 1), (1, 0)])]
    all_to_all x1, starting transfers between devices: 12.4 us -> 9.2 us  [on_device(): parts = lax.all_to_all(sent, PLANE, 0, 0, tiled=True)]
    unnamed x61 -> x32, local copies, waits for them, and re-layouts: 3.92 us -> 2.78 us
  transfers between devices with their start and end apart: 19 -> 19, of which waited for: 8 -> 11; matrix products, arithmetic and copies ran while one was open for 8% -> 9% of each run, Pallas kernels for 1% -> 13%
where the time goes in v3:
time: 147 us; the launch traced here: 146 us
  starting transfers between devices  67.6 us (46%)
  waiting for transfers between devices  38.6 us (26%)
  Pallas kernels  18.5 us (13%)
  local copies, waits for them, and re-layouts  10 us (7%)
  other arithmetic  8.91 us (6%)
  between operations  2.35 us (2%)
    ppermute x8, starting transfers between devices, swap(): return lax.ppermute(x, PAIR, [(0, 1), (1, 0)])  31.3 us
    all_to_all x2, waiting for transfers between devices, from_everyone(): return lax.all_to_all(copies, axis, split_axis=0, concat_axis=0, tiled=True)  16.7 us
    all_to_all x2, starting transfers between devices, from_everyone(): return lax.all_to_all(copies, axis, split_axis=0, concat_axis=0, tiled=True)  12.1 us
    ppermute x7, starting transfers between devices, shifted(): return lax.ppermute(x, FAR, [(i, (i + by) % n) for i in range(n)])  11.4 us
    all_to_all x1, starting transfers between devices, on_device(): parts = lax.all_to_all(sent, PLANE, 0, 0, tiled=True)  9.2 us
    all_to_all x1, waiting for transfers between devices, on_device(): parts = lax.all_to_all(sent, PLANE, 0, 0, tiled=True)  9.11 us
    pallas_call x1, Pallas kernels, attend(): last(meta, own, own, own, other, other, other, prompt, qs, gs, ds, stats,...  8.22 us
    pallas_call x1, Pallas kernels, attend(): ds, stats, prompt_grads = middle(meta, prompt, qs, gs, partial)  7.74 us
  transfers between devices with their start and end apart: 19, of which 11 were waited for; matrix products, arithmetic and copies ran while one was open for 9% of the time, Pallas kernels for 13%

profile of v3, /device:TPU:513, one launch (start us, length us, event | category | flops | bytes accessed | tf_op | source)
XLA Modules:
  0.0 146.3 jit_solution(15023603901369115423)
XLA Ops:
  0.7 0.9 constant_dynamic-slice_fusion.2
  1.6 20.4 %collective-permute-start.3 = (bf16[8,512]{1,0:T(8,128)(2,1)S(1)}, bf16[8,512]{1,0:T(8,128)(2,1)S(1)}, u32[]{:S(2)}, u32[]{:S(2)}) collective-permute-start(bf16[8,512]{1,0:T(8,128)(2,1)S(1)} %pad_maximum_fusion.8), channel_id=1, source_target_pairs={{0,1},{1,0},{2,3},{3,2},{4,5},{5,4},{6,7},{7,6},{8,9},{9,8},{10,11... | collective-permute-start | bytes 24584 | tf_op jit(solution)/shard_map/ppermute | solution.py:26
  22.0 0.7 broadcast_bitcast_fusion
  22.6 0.2 collective-permute-done.3
  22.8 0.1 multiply_reduce_fusion.1
  22.9 0.1 mul.123
  23.1 1.1 broadcast_in_dim.16
  24.2 6.5 %all-to-all-start = ((bf16[64,16,512]{2,1,0:T(8,128)(2,1)}), bf16[64,16,512]{2,1,0:T(8,128)(2,1)S(1)}, u32[]{:S(2)}, u32[]{:S(2)}) async-start(bf16[64,16,512]{2,1,0:T(8,128)(2,1)} %broadcast_in_dim.16), calls=%async_computation | async-start | bytes 2097152 | tf_op jit(solution)/shard_map/all_to_all | solution.py:36
  30.7 1.1 constant_dynamic-slice_fusion.8
  31.9 0.7 constant_dynamic-slice_fusion.6
  32.5 1.1 pad_maximum_fusion.1
  33.7 0.3 collective-permute-start.1
  35.3 0.1 pad_add_fusion
  35.4 0.2 collective-permute-start
  35.7 0.1 constant_dynamic-slice_fusion.5
  35.8 0.6 reshape.88
  36.4 0.3 collective-permute-start.2
  36.8 1.4 pad_maximum_fusion.q_own.g_own.k_own.v_own
  38.2 0.1 pad_add_fusion.1.meta
  38.3 0.8 broadcast_select_fusion.7
  39.2 2.5 %shard_map.138 = (bf16[2,2,1024,128]{3,2,1,0:T(8,128)(2,1)S(1)}, bf16[2,2,1024,128]{3,2,1,0:T(8,128)(2,1)S(1)}, f32[2,2,64,256]{3,2,1,0:T(8,128)S(1)}) custom-call(s32[4]{0:T(128)S(1)} %pad_add_fusion.1.meta, bf16[128,4608]{1,0:T(8,128)(2,1)S(1)} %pad_maximum_fusion.q_own.g_own.k_own.v_own, bf16[128,4608]{1,0:T(8,128)(2,1)S(1)} %pad_maximum_fusion.q_own.g_own.k_own.v_own, ...), custom_call_target="tpu_custom_call" | custom-call | flops 268435456 | bytes 4194304 | tf_op jit(solution)/shard_map/pallas_call | solution.py:305
  41.7 1.0 copy-done.2
  42.7 1.0 copy-done.3
  43.7 0.7 copy-done.8
  44.4 12.8 %all-to-all-done = bf16[64,16,512]{2,1,0:T(8,128)(2,1)S(1)} async-done(((bf16[64,16,512]{2,1,0:T(8,128)(2,1)}), bf16[64,16,512]{2,1,0:T(8,128)(2,1)S(1)}, u32[]{:S(2)}, u32[]{:S(2)}) %all-to-all-start) | async-done | bytes 1048608 | tf_op jit(solution)/shard_map/all_to_all | solution.py:36
  57.2 4.1 %collective-permute-start.7 = (bf16[80,512]{1,0:T(8,128)(2,1)S(1)}, bf16[80,512]{1,0:T(8,128)(2,1)S(1)}, u32[]{:S(2)}, u32[]{:S(2)}) collective-permute-start(bf16[80,512]{1,0:T(8,128)(2,1)S(1)} %pad_maximum_fusion.5.refs_0_), channel_id=1, source_target_pairs={{0,80},{16,96},{32,112},{48,0},{64,16},{80,32},{96,48},{112,64},{1... | collective-permute-start | bytes 245768 | tf_op jit(solution)/shard_map/ppermute | solution.py:31
  61.3 3.3 %collective-permute-start.8 = (bf16[80,512]{1,0:T(8,128)(2,1)S(1)}, bf16[80,512]{1,0:T(8,128)(2,1)S(1)}, u32[]{:S(2)}, u32[]{:S(2)}) collective-permute-start(bf16[80,512]{1,0:T(8,128)(2,1)S(1)} %pad_maximum_fusion.5.refs_0_), channel_id=1, source_target_pairs={{0,96},{16,112},{32,0},{48,16},{64,32},{80,48},{96,64},{112,80},{1... | collective-permute-start | bytes 245768 | tf_op jit(solution)/shard_map/ppermute | solution.py:31
  64.6 0.2 collective-permute-start.10
  64.8 1.6 %collective-permute-start.11 = (bf16[80,512]{1,0:T(8,128)(2,1)S(1)}, bf16[80,512]{1,0:T(8,128)(2,1)S(1)}, u32[]{:S(2)}, u32[]{:S(2)}) collective-permute-start(bf16[80,512]{1,0:T(8,128)(2,1)S(1)} %pad_maximum_fusion.5.refs_0_), channel_id=1, source_target_pairs={{0,32},{16,48},{32,64},{48,80},{64,96},{80,112},{96,0},{112,16},{1... | collective-permute-start | bytes 245768 | tf_op jit(solution)/shard_map/ppermute | solution.py:31
  66.4 0.9 collective-permute-start.12
  67.3 7.7 %shard_map.139 = (bf16[2,2,4,1024,256]{4,3,2,1,0:T(8,128)(2,1)}, f32[2,2,64,256]{3,2,1,0:T(8,128)}, bf16[1024,512]{1,0:T(8,128)(2,1)}) custom-call(s32[4]{0:T(128)} %copy-done.6, bf16[1024,512]{1,0:T(8,128)(2,1)} %bitcast.48, bf16[2,2,1024,128]{3,2,1,0:T(8,128)(2,1)} %copy-done.2, bf16[2,2,1024,128]{3,2,1,0:T(8,128)(2,1)} %copy-done.3, ...), custom_call_target="tpu_custom_call" | custom-call | flops 4294967296 | bytes 12582912 | tf_op jit(solution)/shard_map/pallas_call | solution.py:342
  75.0 1.3 collective-permute-done.11.refs_6_
  76.3 2.4 %collective-permute-done.12.refs_7_ = bf16[80,512]{1,0:T(8,128)(2,1)S(1)} collective-permute-done((bf16[80,512]{1,0:T(8,128)(2,1)S(1)}, bf16[80,512]{1,0:T(8,128)(2,1)S(1)}, u32[]{:S(2)}, u32[]{:S(2)}) %collective-permute-start.12) | collective-permute-done | bytes 81952 | tf_op jit(solution)/shard_map/ppermute | solution.py:31
  78.7 9.2 %all-to-all-start.1 = ((bf16[64,16,512]{2,1,0:T(8,128)(2,1)}), bf16[64,16,512]{2,1,0:T(8,128)(2,1)S(1)}, u32[]{:S(2)}, u32[]{:S(2)}) async-start(bf16[64,16,512]{2,1,0:T(8,128)(2,1)} %bitcast.50), calls=%async_computation.1 | async-start | bytes 2097152 | tf_op jit(solution)/shard_map/all_to_all | solution.py:459
  87.9 8.2 %shard_map.140 = (bf16[128,2048]{1,0:T(8,128)(2,1)}, bf16[128,256]{1,0:T(8,128)(2,1)}, bf16[128,256]{1,0:T(8,128)(2,1)}, bf16[128,2048]{1,0:T(8,128)(2,1)}, bf16...) custom-call(s32[4]{0:T(128)} %copy-done.6, bf16[128,4608]{1,0:T(8,128)(2,1)} %copy-done, bf16[128,4608]{1,0:T(8,128)(2,1)} %copy-done, ...), custom_call_target="tpu_custom_call" | custom-call | flops 2147483648 | bytes 14680064 | tf_op jit(solution)/shard_map/pallas_call | solution.py:356
  96.1 3.7 %collective-permute-start.5 = (bf16[128,256]{1,0:T(8,128)(2,1)}, bf16[128,256]{1,0:T(8,128)(2,1)S(1)}, u32[]{:S(2)}, u32[]{:S(2)}) collective-permute-start(bf16[128,256]{1,0:T(8,128)(2,1)} %get-tuple-element.41), channel_id=1, source_target_pairs={{0,1},{1,0},{2,3},{3,2},{4,5},{5,4},{6,7},{7,6},{8,9},{9,8},{10,11... | collective-permute-start | bytes 196616 | tf_op jit(solution)/shard_map/ppermute | solution.py:26
  99.8 0.2 collective-permute-start.4
  100.0 0.5 collective-permute-start.6
  100.5 0.5 collective-permute-done.5
  100.9 0.9 broadcast_select_fusion.5
  101.8 0.4 collective-permute-done.6
  102.2 0.9 broadcast_select_fusion.3
  103.0 9.1 %all-to-all-done.1 = bf16[64,16,512]{2,1,0:T(8,128)(2,1)S(1)} async-done(((bf16[64,16,512]{2,1,0:T(8,128)(2,1)}), bf16[64,16,512]{2,1,0:T(8,128)(2,1)S(1)}, u32[]{:S(2)}, u32[]{:S(2)}) %all-to-all-start.1) | async-done | bytes 1048608 | tf_op jit(solution)/shard_map/all_to_all | solution.py:459
  112.1 0.2 convert_reduce_fusion
  112.4 0.1 multiply_reduce_fusion
  112.5 0.2 subtract_convert_fusion
  112.8 0.7 broadcast_in_dim.19
  113.4 5.6 %all-to-all-start.2 = ((bf16[8,16,512]{2,1,0:T(8,128)(2,1)}), bf16[8,16,512]{2,1,0:T(8,128)(2,1)S(1)}, u32[]{:S(2)}, u32[]{:S(2)}) async-start(bf16[8,16,512]{2,1,0:T(8,128)(2,1)} %broadcast_in_dim.19), calls=%async_computation.2 | async-start | bytes 262144 | tf_op jit(solution)/shard_map/all_to_all | solution.py:36
  119.0 0.7 pad_maximum_fusion.3
  119.7 1.3 collective-permute-start.13
  121.0 0.7 pad_maximum_fusion.4
  121.7 1.3 collective-permute-done.13.refs_4_
  123.1 3.9 %all-to-all-done.2 = bf16[8,16,512]{2,1,0:T(8,128)(2,1)S(1)} async-done(((bf16[8,16,512]{2,1,0:T(8,128)(2,1)}), bf16[8,16,512]{2,1,0:T(8,128)(2,1)S(1)}, u32[]{:S(2)}, u32[]{:S(2)}) %all-to-all-start.2) | async-done | bytes 131104 | tf_op jit(solution)/shard_map/all_to_all | solution.py:36
  127.0 0.4 fusion.1
  127.3 5.7 %collective-permute-start.14 = (bf16[8,8,640]{2,1,0:T(8,128)(2,1)S(1)}, bf16[8,8,640]{2,1,0:T(8,128)(2,1)S(1)}, u32[]{:S(2)}, u32[]{:S(2)}) collective-permute-start(bf16[8,8,640]{2,1,0:T(8,128)(2,1)S(1)} %fusion.3), channel_id=1, source_target_pairs={{0,1},{1,0},{2,3},{3,2},{4,5},{5,4},{6,7},{7,6},{8,9},{9,8},{10,11... | collective-permute-start | bytes 245768 | tf_op jit(solution)/shard_map/ppermute | solution.py:26
  133.0 0.1 broadcast_select_fusion.1
  133.1 0.8 collective-permute-done.14
  133.9 0.7 fusion
  134.6 3.6 %all-to-all-start.3 = ((bf16[8,8,640]{2,1,0:T(8,128)(2,1)}), bf16[8,8,640]{2,1,0:T(8,128)(2,1)S(1)}, u32[]{:S(2)}, u32[]{:S(2)}) async-start(bf16[8,8,640]{2,1,0:T(8,128)(2,1)} %fusion), calls=%async_computation.3 | async-start | bytes 163840 | tf_op jit(solution)/shard_map/all_to_all | solution.py:478
  138.2 1.0 pad_maximum_fusion.2
  139.2 6.0 %all-to-all-done.3 = bf16[8,8,640]{2,1,0:T(8,128)(2,1)S(1)} async-done(((bf16[8,8,640]{2,1,0:T(8,128)(2,1)}), bf16[8,8,640]{2,1,0:T(8,128)(2,1)S(1)}, u32[]{:S(2)}, u32[]{:S(2)}) %all-to-all-start.3) | async-done | bytes 81952 | tf_op jit(solution)/shard_map/all_to_all | solution.py:478
  145.2 0.2 reshape.96
  145.4 0.1 copy.20
  145.5 0.8 reshape.97
  (61 shorter events, 0.5 us)
Async XLA Ops:
  0.6 30.1 %copy-start.10 = (bf16[128,4096]{1,0:T(8,128)(2,1)S(1)}, bf16[128,4096]{1,0:T(8,128)(2,1)}, u32[]{:S(2)}) copy-start(bf16[128,4096]{1,0:T(8,128)(2,1)} %param.16) | copy-start | bytes 3145732
  0.6 30.1 %copy-start.11 = (bf16[128,4096]{1,0:T(8,128)(2,1)S(1)}, bf16[128,4096]{1,0:T(8,128)(2,1)}, u32[]{:S(2)}) copy-start(bf16[128,4096]{1,0:T(8,128)(2,1)} %param.13) | copy-start | bytes 3145732
  1.6 21.2 %collective-permute-start.3 = (bf16[8,512]{1,0:T(8,128)(2,1)S(1)}, bf16[8,512]{1,0:T(8,128)(2,1)S(1)}, u32[]{:S(2)}, u32[]{:S(2)}) collective-permute-start(bf16[8,512]{1,0:T(8,128)(2,1)S(1)} %pad_maximum_fusion.8), channel_id=1, source_target_pairs={{0,1},{1,0},{2,3},{3,2},{4,5},{5,4},{6,7},{7,6},{8,9},{9,8},{10,11... | collective-permute-start | bytes 24584 | tf_op jit(solution)/shard_map/ppermute | solution.py:26
  24.2 33.0 %all-to-all-start = ((bf16[64,16,512]{2,1,0:T(8,128)(2,1)}), bf16[64,16,512]{2,1,0:T(8,128)(2,1)S(1)}, u32[]{:S(2)}, u32[]{:S(2)}) async-start(bf16[64,16,512]{2,1,0:T(8,128)(2,1)} %broadcast_in_dim.16), calls=%async_computation | async-start | bytes 2097152 | tf_op jit(solution)/shard_map/all_to_all | solution.py:36
  30.7 1.2 copy-start.13
  30.7 1.1 copy-start.14
  31.9 3.8 %copy-start.15 = (bf16[40,1024]{1,0:T(8,128)(2,1)S(1)}, bf16[40,1024]{1,0:T(8,128)(2,1)}, u32[]{:S(2)}) copy-start(bf16[40,1024]{1,0:T(8,128)(2,1)} %param.21) | copy-start | bytes 245764
  33.7 5.5 %copy-start.4 = (f32[128]{0:T(128)S(1)}, f32[128]{0:T(128)}, u32[]{:S(2)}) copy-start(f32[128]{0:T(128)} %param.20) | copy-start | bytes 1540
  33.7 5.5 %copy-start.7 = (f32[128]{0:T(128)S(1)}, f32[128]{0:T(128)}, u32[]{:S(2)}) copy-start(f32[128]{0:T(128)} %param.19) | copy-start | bytes 1540
  33.7 5.5 %collective-permute-start.1 = (bf16[128,4608]{1,0:T(8,128)(2,1)}, bf16[128,4608]{1,0:T(8,128)(2,1)S(1)}, u32[]{:S(2)}, u32[]{:S(2)}) collective-permute-start(bf16[128,4608]{1,0:T(8,128)(2,1)} %pad_maximum_fusion.1), channel_id=1, source_target_pairs={{0,1},{1,0},{2,3},{3,2},{4,5},{5,4},{6,7},{7,6},{8,9},{9,8},{10,11... | collective-permute-start | bytes 3538952 | tf_op jit(solution)/shard_map/ppermute | solution.py:26
  35.4 2.8 %collective-permute-start = (s32[2]{0:T(128)S(1)}, s32[2]{0:T(128)S(1)}, u32[]{:S(2)}, u32[]{:S(2)}) collective-permute-start(s32[2]{0:T(128)S(1)} %pad_add_fusion), channel_id=1, source_target_pairs={{0,1},{1,0},{2,3},{3,2},{4,5},{5,4},{6,7},{7,6},{8,9},{9,8},{10,11... | collective-permute-start | bytes 32 | tf_op jit(solution)/shard_map/ppermute | solution.py:26
  36.4 1.9 %collective-permute-start.2 = (bf16[40,512]{1,0:T(8,128)(2,1)}, bf16[40,512]{1,0:T(8,128)(2,1)}, u32[]{:S(2)}, u32[]{:S(2)}) collective-permute-start(bf16[40,512]{1,0:T(8,128)(2,1)} %reshape.88), channel_id=1, source_target_pairs={{0,1},{1,0},{2,3},{3,2},{4,5},{5,4},{6,7},{7,6},{8,9},{9,8},{10,11... | collective-permute-start | bytes 122888 | tf_op jit(solution)/shard_map/ppermute | solution.py:26
  38.2 3.5 %copy-start = (bf16[128,4608]{1,0:T(8,128)(2,1)}, bf16[128,4608]{1,0:T(8,128)(2,1)S(1)}, u32[]{:S(2)}) copy-start(bf16[128,4608]{1,0:T(8,128)(2,1)S(1)} %pad_maximum_fusion.q_own.g_own.k_own.v_own) | copy-start | bytes 3538948
  38.3 3.4 %copy-start.6 = (s32[4]{0:T(128)}, s32[4]{0:T(128)S(1)}, u32[]{:S(2)}) copy-start(s32[4]{0:T(128)S(1)} %pad_add_fusion.1.meta) | copy-start | bytes 52
  39.1 2.5 %copy-start.1 = (bf16[128,4608]{1,0:T(8,128)(2,1)}, bf16[128,4608]{1,0:T(8,128)(2,1)S(1)}, u32[]{:S(2)}) copy-start(bf16[128,4608]{1,0:T(8,128)(2,1)S(1)} %collective-permute-done.1.q_other.g_other.k_other.v_other) | copy-start | bytes 3538948
  41.7 1.0 copy-start.2
  42.7 1.0 copy-start.3
  43.7 0.7 copy-start.8
  57.2 10.1 %copy-start.9 = (bf16[64,16,512]{2,1,0:T(8,128)(2,1)}, bf16[64,16,512]{2,1,0:T(8,128)(2,1)S(1)}, u32[]{:S(2)}) copy-start(bf16[64,16,512]{2,1,0:T(8,128)(2,1)S(1)} %all-to-all-done) | copy-start | bytes 3145732
  57.2 9.2 %collective-permute-start.7 = (bf16[80,512]{1,0:T(8,128)(2,1)S(1)}, bf16[80,512]{1,0:T(8,128)(2,1)S(1)}, u32[]{:S(2)}, u32[]{:S(2)}) collective-permute-start(bf16[80,512]{1,0:T(8,128)(2,1)S(1)} %pad_maximum_fusion.5.refs_0_), channel_id=1, source_target_pairs={{0,80},{16,96},{32,112},{48,0},{64,16},{80,32},{96,48},{112,64},{1... | collective-permute-start | bytes 245768 | tf_op jit(solution)/shard_map/ppermute | solution.py:31
  61.3 13.7 %collective-permute-start.8 = (bf16[80,512]{1,0:T(8,128)(2,1)S(1)}, bf16[80,512]{1,0:T(8,128)(2,1)S(1)}, u32[]{:S(2)}, u32[]{:S(2)}) collective-permute-start(bf16[80,512]{1,0:T(8,128)(2,1)S(1)} %pad_maximum_fusion.5.refs_0_), channel_id=1, source_target_pairs={{0,96},{16,112},{32,0},{48,16},{64,32},{80,48},{96,64},{112,80},{1... | collective-permute-start | bytes 245768 | tf_op jit(solution)/shard_map/ppermute | solution.py:31
  64.6 10.4 %collective-permute-start.9 = (bf16[80,512]{1,0:T(8,128)(2,1)S(1)}, bf16[80,512]{1,0:T(8,128)(2,1)S(1)}, u32[]{:S(2)}, u32[]{:S(2)}) collective-permute-start(bf16[80,512]{1,0:T(8,128)(2,1)S(1)} %pad_maximum_fusion.5.refs_0_), channel_id=1, source_target_pairs={{0,112},{16,0},{32,16},{48,32},{64,48},{80,64},{96,80},{112,96},{1... | collective-permute-start | bytes 245768 | tf_op jit(solution)/shard_map/ppermute | solution.py:31
  64.6 10.4 %collective-permute-start.10 = (bf16[80,512]{1,0:T(8,128)(2,1)S(1)}, bf16[80,512]{1,0:T(8,128)(2,1)S(1)}, u32[]{:S(2)}, u32[]{:S(2)}) collective-permute-start(bf16[80,512]{1,0:T(8,128)(2,1)S(1)} %pad_maximum_fusion.5.refs_0_), channel_id=1, source_target_pairs={{0,48},{16,64},{32,80},{48,96},{64,112},{80,0},{96,16},{112,32},{1... | collective-permute-start | bytes 245768 | tf_op jit(solution)/shard_map/ppermute | solution.py:31
  64.8 11.5 %collective-permute-start.11 = (bf16[80,512]{1,0:T(8,128)(2,1)S(1)}, bf16[80,512]{1,0:T(8,128)(2,1)S(1)}, u32[]{:S(2)}, u32[]{:S(2)}) collective-permute-start(bf16[80,512]{1,0:T(8,128)(2,1)S(1)} %pad_maximum_fusion.5.refs_0_), channel_id=1, source_target_pairs={{0,32},{16,48},{32,64},{48,80},{64,96},{80,112},{96,0},{112,16},{1... | collective-permute-start | bytes 245768 | tf_op jit(solution)/shard_map/ppermute | solution.py:31
  66.4 12.3 %collective-permute-start.12 = (bf16[80,512]{1,0:T(8,128)(2,1)S(1)}, bf16[80,512]{1,0:T(8,128)(2,1)S(1)}, u32[]{:S(2)}, u32[]{:S(2)}) collective-permute-start(bf16[80,512]{1,0:T(8,128)(2,1)S(1)} %pad_maximum_fusion.5.refs_0_), channel_id=1, source_target_pairs={{0,16},{16,32},{32,48},{48,64},{64,80},{80,96},{96,112},{112,0},{1... | collective-permute-start | bytes 245768 | tf_op jit(solution)/shard_map/ppermute | solution.py:31
  78.7 33.4 %all-to-all-start.1 = ((bf16[64,16,512]{2,1,0:T(8,128)(2,1)}), bf16[64,16,512]{2,1,0:T(8,128)(2,1)S(1)}, u32[]{:S(2)}, u32[]{:S(2)}) async-start(bf16[64,16,512]{2,1,0:T(8,128)(2,1)} %bitcast.50), calls=%async_computation.1 | async-start | bytes 2097152 | tf_op jit(solution)/shard_map/all_to_all | solution.py:459
  87.9 24.5 %copy-start.5 = (f32[128]{0:T(128)S(1)}, f32[128]{0:T(128)}, u32[]{:S(2)}) copy-start(f32[128]{0:T(128)} %param.20) | copy-start | bytes 1540
  96.1 4.8 %collective-permute-start.5 = (bf16[128,256]{1,0:T(8,128)(2,1)}, bf16[128,256]{1,0:T(8,128)(2,1)S(1)}, u32[]{:S(2)}, u32[]{:S(2)}) collective-permute-start(bf16[128,256]{1,0:T(8,128)(2,1)} %get-tuple-element.41), channel_id=1, source_target_pairs={{0,1},{1,0},{2,3},{3,2},{4,5},{5,4},{6,7},{7,6},{8,9},{9,8},{10,11... | collective-permute-start | bytes 196616 | tf_op jit(solution)/shard_map/ppermute | solution.py:26
  99.8 33.2 %collective-permute-start.4 = (bf16[128,2048]{1,0:T(8,128)(2,1)}, bf16[128,2048]{1,0:T(8,128)(2,1)S(1)}, u32[]{:S(2)}, u32[]{:S(2)}) collective-permute-start(bf16[128,2048]{1,0:T(8,128)(2,1)} %get-tuple-element.39), channel_id=1, source_target_pairs={{0,1},{1,0},{2,3},{3,2},{4,5},{5,4},{6,7},{7,6},{8,9},{9,8},{10,11... | collective-permute-start | bytes 1572872 | tf_op jit(solution)/shard_map/ppermute | solution.py:26
  100.0 2.2 %collective-permute-start.6 = (bf16[128,256]{1,0:T(8,128)(2,1)}, bf16[128,256]{1,0:T(8,128)(2,1)S(1)}, u32[]{:S(2)}, u32[]{:S(2)}) collective-permute-start(bf16[128,256]{1,0:T(8,128)(2,1)} %get-tuple-element.43), channel_id=1, source_target_pairs={{0,1},{1,0},{2,3},{3,2},{4,5},{5,4},{6,7},{7,6},{8,9},{9,8},{10,11... | collective-permute-start | bytes 196616 | tf_op jit(solution)/shard_map/ppermute | solution.py:26
  112.3 20.7 %copy-start.12 = (bf16[128,2048]{1,0:T(8,128)(2,1)S(1)}, bf16[128,2048]{1,0:T(8,128)(2,1)}, u32[]{:S(2)}) copy-start(bf16[128,2048]{1,0:T(8,128)(2,1)} %get-tuple-element.38) | copy-start | bytes 1572868
  113.4 13.5 %all-to-all-start.2 = ((bf16[8,16,512]{2,1,0:T(8,128)(2,1)}), bf16[8,16,512]{2,1,0:T(8,128)(2,1)S(1)}, u32[]{:S(2)}, u32[]{:S(2)}) async-start(bf16[8,16,512]{2,1,0:T(8,128)(2,1)} %broadcast_in_dim.19), calls=%async_computation.2 | async-start | bytes 262144 | tf_op jit(solution)/shard_map/all_to_all | solution.py:36
  119.7 3.3 %collective-permute-start.13 = (bf16[80,512]{1,0:T(8,128)(2,1)S(1)}, bf16[80,512]{1,0:T(8,128)(2,1)S(1)}, u32[]{:S(2)}, u32[]{:S(2)}) collective-permute-start(bf16[80,512]{1,0:T(8,128)(2,1)S(1)} %collective-permute-done.7.refs_3_), channel_id=1, source_target_pairs={{0,112},{16,0},{32,16},{48,32},{64,48},{80,64},{96,80},{112,96},{1... | collective-permute-start | bytes 245768 | tf_op jit(solution)/shard_map/ppermute | solution.py:31
  127.3 6.6 %collective-permute-start.14 = (bf16[8,8,640]{2,1,0:T(8,128)(2,1)S(1)}, bf16[8,8,640]{2,1,0:T(8,128)(2,1)S(1)}, u32[]{:S(2)}, u32[]{:S(2)}) collective-permute-start(bf16[8,8,640]{2,1,0:T(8,128)(2,1)S(1)} %fusion.3), channel_id=1, source_target_pairs={{0,1},{1,0},{2,3},{3,2},{4,5},{5,4},{6,7},{7,6},{8,9},{9,8},{10,11... | collective-permute-start | bytes 245768 | tf_op jit(solution)/shard_map/ppermute | solution.py:26
  134.6 10.6 %all-to-all-start.3 = ((bf16[8,8,640]{2,1,0:T(8,128)(2,1)}), bf16[8,8,640]{2,1,0:T(8,128)(2,1)S(1)}, u32[]{:S(2)}, u32[]{:S(2)}) async-start(bf16[8,8,640]{2,1,0:T(8,128)(2,1)} %fusion), calls=%async_computation.3 | async-start | bytes 163840 | tf_op jit(solution)/shard_map/all_to_all | solution.py:478

commit v4 on v3

--- a/solution.py
+++ b/solution.py
@@ -302,18 +302,17 @@
     def shaped(shape, kind):
         return jax.ShapeDtypeStruct((heads, 2, *shape), kind)
 
-    qs, gs, partial = pl.pallas_call(
+    before = pl.pallas_call(
         before_kernel,
         grid=(heads,),
         in_specs=[scalars, q_side, g_side, k_side, v_side, q_side, g_side, k_side, v_side, gain, gain],
         out_specs=[by_pair(*stack), by_pair(*stack), by_pair(*stat)],
         out_shape=[shaped(stack, low), shaped(stack, low), shaped(stat, high)],
-        compiler_params=limit(8),
+        compiler_params=limit(60),
         cost_estimate=cost(2, slots, 4 * 1024 * 1024),
-    )(meta, own, own, own, own, other, other, other, other, q_gain, k_gain)
-    weight_pair, prompt, qs, gs, partial = lax.optimization_barrier(
-        (weight_pair, prompt, qs, gs, partial)
-    )
+    )
+    qs, gs, partial = before(meta, own, own, own, own, other, other, other, other, q_gain, k_gain)
+    prompt, qs, gs, partial = lax.optimization_barrier((prompt, qs, gs, partial))
     above, below = [], []
     for k in NEARBY:
         below.append(shifted(weight_pair, k))

time: 147 us -> 142 us (0.966)
  waiting for transfers between devices: 38.6 us -> 18.3 us
  starting transfers between devices: 67.6 us -> 81.5 us
  local copies, waits for them, and re-layouts: 10 us -> 7.95 us
  Pallas kernels: 18.5 us -> 20.2 us
    ppermute x7, starting transfers between devices: 11.4 us -> 20.2 us  [shifted(): return lax.ppermute(x, FAR, [(i, (i + by) % n) for i in range(n)])]
    all_to_all x1, waiting for transfers between devices: 9.11 us -> 1.63 us  [on_device(): parts = lax.all_to_all(sent, PLANE, 0, 0, tiled=True)]
    all_to_all x2, waiting for transfers between devices: 16.7 us -> 9.69 us  [from_everyone(): return lax.all_to_all(copies, axis, split_axis=0, concat_axis=0, tiled=True)]
    ppermute x7, waiting for transfers between devices: 5 us -> 0.02 us  [shifted(): return lax.ppermute(x, FAR, [(i, (i + by) % n) for i in range(n)])]
    unnamed x32 -> x18, local copies, waits for them, and re-layouts: 2.78 us -> 0.04 us
    all_to_all x1, starting transfers between devices: 9.2 us -> 11.6 us  [on_device(): parts = lax.all_to_all(sent, PLANE, 0, 0, tiled=True)]
    ppermute x8, starting transfers between devices: 31.3 us -> 33 us  [swap(): return lax.ppermute(x, PAIR, [(0, 1), (1, 0)])]
    pallas_call x1, Pallas kernels: 2.46 us -> 4.01 us  [attend(): before(meta, own, own, own, own, other, other, other, other, q_gain, k_gain)]
  transfers between devices with their start and end apart: 19 -> 19, of which waited for: 11 -> 6; matrix products, arithmetic and copies ran while one was open for 9% -> 10% of each run, Pallas kernels for 13% -> 14%
where the time goes in v4:
time: 142 us; the launch traced here: 140 us
  starting transfers between devices  81.5 us (57%)
  Pallas kernels  20.2 us (14%)
  waiting for transfers between devices  18.3 us (13%)
  other arithmetic  9.78 us (7%)
  local copies, waits for them, and re-layouts  7.95 us (6%)
  between operations  2.32 us (2%)
    ppermute x8, starting transfers between devices, swap(): return lax.ppermute(x, PAIR, [(0, 1), (1, 0)])  33 us
    ppermute x7, starting transfers between devices, shifted(): return lax.ppermute(x, FAR, [(i, (i + by) % n) for i in range(n)])  20.2 us
    all_to_all x2, starting transfers between devices, from_everyone(): return lax.all_to_all(copies, axis, split_axis=0, concat_axis=0, tiled=True)  13.2 us
    all_to_all x1, starting transfers between devices, on_device(): parts = lax.all_to_all(sent, PLANE, 0, 0, tiled=True)  11.6 us
    all_to_all x2, waiting for transfers between devices, from_everyone(): return lax.all_to_all(copies, axis, split_axis=0, concat_axis=0, tiled=True)  9.69 us
    pallas_call x1, Pallas kernels, attend(): last(meta, own, own, own, other, other, other, prompt, qs, gs, ds, stats,...  8.34 us
    pallas_call x1, Pallas kernels, attend(): ds, stats, prompt_grads = middle(meta, prompt, qs, gs, partial)  7.75 us
    all_to_all x1, waiting for transfers between devices, on_device(): arrived = lax.all_to_all(mine, NEAR, 0, 0, tiled=True)  5.98 us
  transfers between devices with their start and end apart: 19, of which 6 were waited for; matrix products, arithmetic and copies ran while one was open for 10% of the time, Pallas kernels for 14%

profile of v4, /device:TPU:513, one launch (start us, length us, event | category | flops | bytes accessed | tf_op | source)
XLA Modules:
  0.0 140.4 jit_solution(11761776734529480409)
XLA Ops:
  0.6 0.7 constant_dynamic-slice_fusion.4
  1.4 20.4 %collective-permute-start.2 = (bf16[8,512]{1,0:T(8,128)(2,1)S(1)}, bf16[8,512]{1,0:T(8,128)(2,1)S(1)}, u32[]{:S(2)}, u32[]{:S(2)}) collective-permute-start(bf16[8,512]{1,0:T(8,128)(2,1)S(1)} %pad_maximum_fusion.8), channel_id=1, source_target_pairs={{0,1},{1,0},{2,3},{3,2},{4,5},{5,4},{6,7},{7,6},{8,9},{9,8},{10,11... | collective-permute-start | bytes 24584 | tf_op jit(solution)/shard_map/ppermute | solution.py:26
  21.8 0.7 broadcast_bitcast_fusion
  22.5 0.2 collective-permute-done.2
  22.7 0.1 multiply_reduce_fusion.1
  22.8 0.6 multiply_multiply_fusion
  23.4 0.1 mul.123
  23.5 1.1 broadcast_in_dim.16
  24.6 6.5 %all-to-all-start = ((bf16[64,16,512]{2,1,0:T(8,128)(2,1)}), bf16[64,16,512]{2,1,0:T(8,128)(2,1)S(1)}, u32[]{:S(2)}, u32[]{:S(2)}) async-start(bf16[64,16,512]{2,1,0:T(8,128)(2,1)} %broadcast_in_dim.16), calls=%async_computation | async-start | bytes 2097152 | tf_op jit(solution)/shard_map/all_to_all | solution.py:36
  31.1 0.0 copy-start.3
  31.1 0.0 copy-start.4
  31.1 1.7 %constant_dynamic-slice_fusion.8 = (bf16[128,2048]{1,0:T(8,128)(2,1)S(1)}, bf16[128,2048]{1,0:T(8,128)(2,1)S(1)}, bf16[128,2048]{1,0:T(8,128)(2,1)S(1)}, bf16[128,2048]{1,0:T(8,128)(2,1)S(1)}) fusion(bf16[128,4096]{1,0:T(8,128)(2,1)} %param.16, s32[]{:T(128)S(6)} %select_n.89, s32[]{:T(128)S(6)} %select_n.87, bf16[128,4096]{1,0:T(8,128)(2,1)} %param.13), kind=kLoop, calls=%fused_computation.58 | loop fusion | bytes 4194312 | tf_op jit(solution)/shard_map/dynamic_slice | solution.py:385
  32.9 0.7 constant_dynamic-slice_fusion.6
  33.5 1.1 pad_maximum_fusion.1
  34.6 0.3 collective-permute-start.1
  36.3 0.1 pad_add_fusion
  36.4 0.2 collective-permute-start
  36.6 0.9 reshape.88
  37.5 0.1 constant_dynamic-slice_fusion.1
  37.7 0.5 collective-permute-start.6
  38.1 2.0 %pad_maximum_fusion.q_own.g_own.k_own.v_own = bf16[128,4608]{1,0:T(8,128)(2,1)} fusion(bf16[128,256]{1,0:T(8,128)(2,1)S(1)} %get-tuple-element.65, bf16[128,256]{1,0:T(8,128)(2,1)} %get-tuple-element.82, bf16[128,2048]{1,0:T(8,128)(2,1)S(1)} %get-tuple-element.57, bf16[128,2048]{1,0:T(8,128)(2,1)S(1)} %get-tuple-element.84), kind=kLoop, calls=%fused_computation.1 | loop fusion | flops 4718592 | bytes 2359296 | tf_op jit(solution)/shard_map/concatenate | solution.py:397
  40.1 0.0 collective-permute-done.6
  40.2 4.0 %collective-permute-start.7 = (bf16[80,512]{1,0:T(8,128)(2,1)S(1)}, bf16[80,512]{1,0:T(8,128)(2,1)S(1)}, u32[]{:S(2)}, u32[]{:S(2)}) collective-permute-start(bf16[80,512]{1,0:T(8,128)(2,1)S(1)} %pad_maximum_fusion.5.refs_0_), channel_id=1, source_target_pairs={{0,80},{16,96},{32,112},{48,0},{64,16},{80,32},{96,48},{112,64},{1... | collective-permute-start | bytes 245768 | tf_op jit(solution)/shard_map/ppermute | solution.py:31
  44.2 0.6 pad_add_fusion.1.meta
  44.8 0.9 collective-permute-start.8
  45.6 0.2 collective-permute-start.9
  45.8 2.5 %collective-permute-start.10 = (bf16[80,512]{1,0:T(8,128)(2,1)S(1)}, bf16[80,512]{1,0:T(8,128)(2,1)S(1)}, u32[]{:S(2)}, u32[]{:S(2)}) collective-permute-start(bf16[80,512]{1,0:T(8,128)(2,1)S(1)} %pad_maximum_fusion.5.refs_0_), channel_id=1, source_target_pairs={{0,48},{16,64},{32,80},{48,96},{64,112},{80,0},{96,16},{112,32},{1... | collective-permute-start | bytes 245768 | tf_op jit(solution)/shard_map/ppermute | solution.py:31
  48.3 1.8 %collective-permute-start.11 = (bf16[80,512]{1,0:T(8,128)(2,1)S(1)}, bf16[80,512]{1,0:T(8,128)(2,1)S(1)}, u32[]{:S(2)}, u32[]{:S(2)}) collective-permute-start(bf16[80,512]{1,0:T(8,128)(2,1)S(1)} %pad_maximum_fusion.5.refs_0_), channel_id=1, source_target_pairs={{0,32},{16,48},{32,64},{48,80},{64,96},{80,112},{96,0},{112,16},{1... | collective-permute-start | bytes 245768 | tf_op jit(solution)/shard_map/ppermute | solution.py:31
  50.1 4.0 %shard_map.138 = (bf16[2,2,1024,128]{3,2,1,0:T(8,128)(2,1)}, bf16[2,2,1024,128]{3,2,1,0:T(8,128)(2,1)}, f32[2,2,64,256]{3,2,1,0:T(8,128)}) custom-call(s32[4]{0:T(128)} %pad_add_fusion.1.meta, bf16[128,4608]{1,0:T(8,128)(2,1)} %pad_maximum_fusion.q_own.g_own.k_own.v_own, bf16[128,4608]{1,0:T(8,128)(2,1)} %pad_maximum_fusion.q_own.g_own.k_own.v_own, ...), custom_call_target="tpu_custom_call" | custom-call | flops 268435456 | bytes 4194304 | tf_op jit(solution)/shard_map/pallas_call | solution.py:314
  54.1 3.2 %all-to-all-done = bf16[64,16,512]{2,1,0:T(8,128)(2,1)S(1)} async-done(((bf16[64,16,512]{2,1,0:T(8,128)(2,1)}), bf16[64,16,512]{2,1,0:T(8,128)(2,1)S(1)}, u32[]{:S(2)}, u32[]{:S(2)}) %all-to-all-start) | async-done | bytes 1048608 | tf_op jit(solution)/shard_map/all_to_all | solution.py:36
  57.3 5.3 %collective-permute-start.12 = (bf16[80,512]{1,0:T(8,128)(2,1)S(1)}, bf16[80,512]{1,0:T(8,128)(2,1)S(1)}, u32[]{:S(2)}, u32[]{:S(2)}) collective-permute-start(bf16[80,512]{1,0:T(8,128)(2,1)S(1)} %pad_maximum_fusion.5.refs_0_), channel_id=1, source_target_pairs={{0,16},{16,32},{32,48},{48,64},{64,80},{80,96},{96,112},{112,0},{1... | collective-permute-start | bytes 245768 | tf_op jit(solution)/shard_map/ppermute | solution.py:31
  62.6 7.7 %shard_map.139 = (bf16[2,2,4,1024,256]{4,3,2,1,0:T(8,128)(2,1)}, f32[2,2,64,256]{3,2,1,0:T(8,128)}, bf16[1024,512]{1,0:T(8,128)(2,1)}) custom-call(s32[4]{0:T(128)} %pad_add_fusion.1.meta, bf16[1024,512]{1,0:T(8,128)(2,1)} %bitcast.44, bf16[2,2,1024,128]{3,2,1,0:T(8,128)(2,1)} %get-tuple-element.32.qs, bf16[2,2,1024,128]{3,2,1,0:T(8,128)(2,1)} %get-tuple-element.33.gs, ...), custom_call_target="tpu_custom_call" | custom-call | flops 4294967296 | bytes 12582912 | tf_op jit(solution)/shard_map/pallas_call | solution.py:341
  70.4 0.0 collective-permute-done.8.refs_2_
  70.4 0.0 collective-permute-done.10.refs_5_
  70.4 11.6 %all-to-all-start.1 = ((bf16[64,16,512]{2,1,0:T(8,128)(2,1)}), bf16[64,16,512]{2,1,0:T(8,128)(2,1)S(1)}, u32[]{:S(2)}, u32[]{:S(2)}) async-start(bf16[64,16,512]{2,1,0:T(8,128)(2,1)} %bitcast.46), calls=%async_computation.1 | async-start | bytes 2097152 | tf_op jit(solution)/shard_map/all_to_all | solution.py:458
  82.0 0.0 copy-start.8
  82.1 8.3 %shard_map.140 = (bf16[128,2048]{1,0:T(8,128)(2,1)}, bf16[128,256]{1,0:T(8,128)(2,1)}, bf16[128,256]{1,0:T(8,128)(2,1)}, bf16[128,2048]{1,0:T(8,128)(2,1)}, bf16...) custom-call(s32[4]{0:T(128)} %pad_add_fusion.1.meta, bf16[128,4608]{1,0:T(8,128)(2,1)} %pad_maximum_fusion.q_own.g_own.k_own.v_own, ...), custom_call_target="tpu_custom_call" | custom-call | flops 2147483648 | bytes 14680064 | tf_op jit(solution)/shard_map/pallas_call | solution.py:355
  90.4 4.6 %collective-permute-start.4 = (bf16[128,256]{1,0:T(8,128)(2,1)}, bf16[128,256]{1,0:T(8,128)(2,1)S(1)}, u32[]{:S(2)}, u32[]{:S(2)}) collective-permute-start(bf16[128,256]{1,0:T(8,128)(2,1)} %get-tuple-element.40), channel_id=1, source_target_pairs={{0,1},{1,0},{2,3},{3,2},{4,5},{5,4},{6,7},{7,6},{8,9},{9,8},{10,11... | collective-permute-start | bytes 196616 | tf_op jit(solution)/shard_map/ppermute | solution.py:26
  95.1 0.2 collective-permute-start.3
  95.2 0.5 collective-permute-start.5
  95.7 5.5 %collective-permute-start.13 = (bf16[80,512]{1,0:T(8,128)(2,1)S(1)}, bf16[80,512]{1,0:T(8,128)(2,1)S(1)}, u32[]{:S(2)}, u32[]{:S(2)}) collective-permute-start(bf16[80,512]{1,0:T(8,128)(2,1)S(1)} %collective-permute-done.7.refs_3_), channel_id=1, source_target_pairs={{0,112},{16,0},{32,16},{48,32},{64,48},{80,64},{96,80},{112,96},{1... | collective-permute-start | bytes 245768 | tf_op jit(solution)/shard_map/ppermute | solution.py:31
  101.2 0.9 broadcast_select_fusion.5
  102.1 0.9 broadcast_select_fusion.3
  102.9 1.6 %all-to-all-done.1 = bf16[64,16,512]{2,1,0:T(8,128)(2,1)S(1)} async-done(((bf16[64,16,512]{2,1,0:T(8,128)(2,1)}), bf16[64,16,512]{2,1,0:T(8,128)(2,1)S(1)}, u32[]{:S(2)}, u32[]{:S(2)}) %all-to-all-start.1) | async-done | bytes 1048608 | tf_op jit(solution)/shard_map/all_to_all | solution.py:458
  104.6 0.2 convert_reduce_fusion
  104.8 0.1 multiply_reduce_fusion
  105.0 0.2 subtract_convert_fusion
  105.2 0.7 broadcast_in_dim.19
  105.9 6.7 %all-to-all-start.2 = ((bf16[8,16,512]{2,1,0:T(8,128)(2,1)}), bf16[8,16,512]{2,1,0:T(8,128)(2,1)S(1)}, u32[]{:S(2)}, u32[]{:S(2)}) async-start(bf16[8,16,512]{2,1,0:T(8,128)(2,1)} %broadcast_in_dim.19), calls=%async_computation.2 | async-start | bytes 262144 | tf_op jit(solution)/shard_map/all_to_all | solution.py:36
  112.6 0.7 pad_maximum_fusion.3
  113.3 0.7 pad_maximum_fusion.4
  113.9 0.1 shard_map.141
  114.0 6.5 %all-to-all-done.2 = bf16[8,16,512]{2,1,0:T(8,128)(2,1)S(1)} async-done(((bf16[8,16,512]{2,1,0:T(8,128)(2,1)}), bf16[8,16,512]{2,1,0:T(8,128)(2,1)S(1)}, u32[]{:S(2)}, u32[]{:S(2)}) %all-to-all-start.2) | async-done | bytes 131104 | tf_op jit(solution)/shard_map/all_to_all | solution.py:36
  120.5 0.4 fusion.1
  120.9 6.3 %collective-permute-start.14 = (bf16[8,8,640]{2,1,0:T(8,128)(2,1)S(1)}, bf16[8,8,640]{2,1,0:T(8,128)(2,1)S(1)}, u32[]{:S(2)}, u32[]{:S(2)}) collective-permute-start(bf16[8,8,640]{2,1,0:T(8,128)(2,1)S(1)} %fusion.3), channel_id=1, source_target_pairs={{0,1},{1,0},{2,3},{3,2},{4,5},{5,4},{6,7},{7,6},{8,9},{9,8},{10,11... | collective-permute-start | bytes 245768 | tf_op jit(solution)/shard_map/ppermute | solution.py:26
  127.2 0.1 broadcast_select_fusion.1
  127.3 0.8 collective-permute-done.14
  128.1 0.7 fusion
  128.7 3.6 %all-to-all-start.3 = ((bf16[8,8,640]{2,1,0:T(8,128)(2,1)}), bf16[8,8,640]{2,1,0:T(8,128)(2,1)S(1)}, u32[]{:S(2)}, u32[]{:S(2)}) async-start(bf16[8,8,640]{2,1,0:T(8,128)(2,1)} %fusion), calls=%async_computation.3 | async-start | bytes 163840 | tf_op jit(solution)/shard_map/all_to_all | solution.py:477
  132.3 1.0 pad_maximum_fusion.2
  133.4 6.0 %all-to-all-done.3 = bf16[8,8,640]{2,1,0:T(8,128)(2,1)S(1)} async-done(((bf16[8,8,640]{2,1,0:T(8,128)(2,1)}), bf16[8,8,640]{2,1,0:T(8,128)(2,1)S(1)}, u32[]{:S(2)}, u32[]{:S(2)}) %all-to-all-start.3) | async-done | bytes 81952 | tf_op jit(solution)/shard_map/all_to_all | solution.py:477
  139.3 0.2 reshape.96
  139.5 0.1 copy.20
  139.6 0.8 reshape.97
  (47 shorter events, 0.4 us)
Async XLA Ops:
  1.4 21.2 %collective-permute-start.2 = (bf16[8,512]{1,0:T(8,128)(2,1)S(1)}, bf16[8,512]{1,0:T(8,128)(2,1)S(1)}, u32[]{:S(2)}, u32[]{:S(2)}) collective-permute-start(bf16[8,512]{1,0:T(8,128)(2,1)S(1)} %pad_maximum_fusion.8), channel_id=1, source_target_pairs={{0,1},{1,0},{2,3},{3,2},{4,5},{5,4},{6,7},{7,6},{8,9},{9,8},{10,11... | collective-permute-start | bytes 24584 | tf_op jit(solution)/shard_map/ppermute | solution.py:26
  23.4 1.2 copy-start.5
  24.6 32.7 %all-to-all-start = ((bf16[64,16,512]{2,1,0:T(8,128)(2,1)}), bf16[64,16,512]{2,1,0:T(8,128)(2,1)S(1)}, u32[]{:S(2)}, u32[]{:S(2)}) async-start(bf16[64,16,512]{2,1,0:T(8,128)(2,1)} %broadcast_in_dim.16), calls=%async_computation | async-start | bytes 2097152 | tf_op jit(solution)/shard_map/all_to_all | solution.py:36
  31.1 1.7 %copy-start.3 = (bf16[128,512]{1,0:T(8,128)(2,1)S(1)}, bf16[128,512]{1,0:T(8,128)(2,1)}, u32[]{:S(2)}) copy-start(bf16[128,512]{1,0:T(8,128)(2,1)} %param.15) | copy-start | bytes 393220
  31.1 1.7 %copy-start.4 = (bf16[128,512]{1,0:T(8,128)(2,1)S(1)}, bf16[128,512]{1,0:T(8,128)(2,1)}, u32[]{:S(2)}) copy-start(bf16[128,512]{1,0:T(8,128)(2,1)} %param.14) | copy-start | bytes 393220
  34.6 13.7 %collective-permute-start.1 = (bf16[128,4608]{1,0:T(8,128)(2,1)}, bf16[128,4608]{1,0:T(8,128)(2,1)S(1)}, u32[]{:S(2)}, u32[]{:S(2)}) collective-permute-start(bf16[128,4608]{1,0:T(8,128)(2,1)} %pad_maximum_fusion.1), channel_id=1, source_target_pairs={{0,1},{1,0},{2,3},{3,2},{4,5},{5,4},{6,7},{7,6},{8,9},{9,8},{10,11... | collective-permute-start | bytes 3538952 | tf_op jit(solution)/shard_map/ppermute | solution.py:26
  36.4 7.8 %collective-permute-start = (s32[2]{0:T(128)S(1)}, s32[2]{0:T(128)S(1)}, u32[]{:S(2)}, u32[]{:S(2)}) collective-permute-start(s32[2]{0:T(128)S(1)} %pad_add_fusion), channel_id=1, source_target_pairs={{0,1},{1,0},{2,3},{3,2},{4,5},{5,4},{6,7},{7,6},{8,9},{9,8},{10,11... | collective-permute-start | bytes 32 | tf_op jit(solution)/shard_map/ppermute | solution.py:26
  37.7 2.5 %collective-permute-start.6 = (bf16[40,512]{1,0:T(8,128)(2,1)S(1)}, bf16[40,512]{1,0:T(8,128)(2,1)S(1)}, u32[]{:S(2)}, u32[]{:S(2)}) collective-permute-start(bf16[40,512]{1,0:T(8,128)(2,1)S(1)} %reshape.90), channel_id=1, source_target_pairs={{0,1},{1,0},{2,3},{3,2},{4,5},{5,4},{6,7},{7,6},{8,9},{9,8},{10,11... | collective-permute-start | bytes 122888 | tf_op jit(solution)/shard_map/ppermute | solution.py:26
  40.2 17.1 %collective-permute-start.7 = (bf16[80,512]{1,0:T(8,128)(2,1)S(1)}, bf16[80,512]{1,0:T(8,128)(2,1)S(1)}, u32[]{:S(2)}, u32[]{:S(2)}) collective-permute-start(bf16[80,512]{1,0:T(8,128)(2,1)S(1)} %pad_maximum_fusion.5.refs_0_), channel_id=1, source_target_pairs={{0,80},{16,96},{32,112},{48,0},{64,16},{80,32},{96,48},{112,64},{1... | collective-permute-start | bytes 245768 | tf_op jit(solution)/shard_map/ppermute | solution.py:31
  44.8 25.6 %collective-permute-start.8 = (bf16[80,512]{1,0:T(8,128)(2,1)S(1)}, bf16[80,512]{1,0:T(8,128)(2,1)S(1)}, u32[]{:S(2)}, u32[]{:S(2)}) collective-permute-start(bf16[80,512]{1,0:T(8,128)(2,1)S(1)} %pad_maximum_fusion.5.refs_0_), channel_id=1, source_target_pairs={{0,96},{16,112},{32,0},{48,16},{64,32},{80,48},{96,64},{112,80},{1... | collective-permute-start | bytes 245768 | tf_op jit(solution)/shard_map/ppermute | solution.py:31
  45.6 24.8 %collective-permute-start.9 = (bf16[80,512]{1,0:T(8,128)(2,1)S(1)}, bf16[80,512]{1,0:T(8,128)(2,1)S(1)}, u32[]{:S(2)}, u32[]{:S(2)}) collective-permute-start(bf16[80,512]{1,0:T(8,128)(2,1)S(1)} %pad_maximum_fusion.5.refs_0_), channel_id=1, source_target_pairs={{0,112},{16,0},{32,16},{48,32},{64,48},{80,64},{96,80},{112,96},{1... | collective-permute-start | bytes 245768 | tf_op jit(solution)/shard_map/ppermute | solution.py:31
  45.8 24.6 %collective-permute-start.10 = (bf16[80,512]{1,0:T(8,128)(2,1)S(1)}, bf16[80,512]{1,0:T(8,128)(2,1)S(1)}, u32[]{:S(2)}, u32[]{:S(2)}) collective-permute-start(bf16[80,512]{1,0:T(8,128)(2,1)S(1)} %pad_maximum_fusion.5.refs_0_), channel_id=1, source_target_pairs={{0,48},{16,64},{32,80},{48,96},{64,112},{80,0},{96,16},{112,32},{1... | collective-permute-start | bytes 245768 | tf_op jit(solution)/shard_map/ppermute | solution.py:31
  48.3 1.8 %copy-start = (bf16[128,4608]{1,0:T(8,128)(2,1)}, bf16[128,4608]{1,0:T(8,128)(2,1)S(1)}, u32[]{:S(2)}) copy-start(bf16[128,4608]{1,0:T(8,128)(2,1)S(1)} %collective-permute-done.1.q_other.g_other.k_other.v_other) | copy-start | bytes 3538948
  48.3 22.1 %collective-permute-start.11 = (bf16[80,512]{1,0:T(8,128)(2,1)S(1)}, bf16[80,512]{1,0:T(8,128)(2,1)S(1)}, u32[]{:S(2)}, u32[]{:S(2)}) collective-permute-start(bf16[80,512]{1,0:T(8,128)(2,1)S(1)} %pad_maximum_fusion.5.refs_0_), channel_id=1, source_target_pairs={{0,32},{16,48},{32,64},{48,80},{64,96},{80,112},{96,0},{112,16},{1... | collective-permute-start | bytes 245768 | tf_op jit(solution)/shard_map/ppermute | solution.py:31
  57.3 5.3 %copy-start.1 = (bf16[64,16,512]{2,1,0:T(8,128)(2,1)}, bf16[64,16,512]{2,1,0:T(8,128)(2,1)S(1)}, u32[]{:S(2)}) copy-start(bf16[64,16,512]{2,1,0:T(8,128)(2,1)S(1)} %all-to-all-done) | copy-start | bytes 3145732
  57.3 13.1 %collective-permute-start.12 = (bf16[80,512]{1,0:T(8,128)(2,1)S(1)}, bf16[80,512]{1,0:T(8,128)(2,1)S(1)}, u32[]{:S(2)}, u32[]{:S(2)}) collective-permute-start(bf16[80,512]{1,0:T(8,128)(2,1)S(1)} %pad_maximum_fusion.5.refs_0_), channel_id=1, source_target_pairs={{0,16},{16,32},{32,48},{48,64},{64,80},{80,96},{96,112},{112,0},{1... | collective-permute-start | bytes 245768 | tf_op jit(solution)/shard_map/ppermute | solution.py:31
  70.4 34.1 %all-to-all-start.1 = ((bf16[64,16,512]{2,1,0:T(8,128)(2,1)}), bf16[64,16,512]{2,1,0:T(8,128)(2,1)S(1)}, u32[]{:S(2)}, u32[]{:S(2)}) async-start(bf16[64,16,512]{2,1,0:T(8,128)(2,1)} %bitcast.46), calls=%async_computation.1 | async-start | bytes 2097152 | tf_op jit(solution)/shard_map/all_to_all | solution.py:458
  82.0 22.8 %copy-start.8 = (f32[128]{0:T(128)S(1)}, f32[128]{0:T(128)}, u32[]{:S(2)}) copy-start(f32[128]{0:T(128)} %param.20) | copy-start | bytes 1540
  82.1 22.9 %copy-start.6 = (f32[16,2]{1,0:T(8,128)S(1)}, f32[16,2]{1,0:T(8,128)}, u32[]{:S(2)}) copy-start(f32[16,2]{1,0:T(8,128)} %copy-done.5) | copy-start | bytes 388
  82.1 22.9 %copy-start.7 = (f32[16,2]{1,0:T(8,128)S(1)}, f32[16,2]{1,0:T(8,128)}, u32[]{:S(2)}) copy-start(f32[16,2]{1,0:T(8,128)} %get-tuple-element.72) | copy-start | bytes 388
  90.4 10.8 %collective-permute-start.4 = (bf16[128,256]{1,0:T(8,128)(2,1)}, bf16[128,256]{1,0:T(8,128)(2,1)S(1)}, u32[]{:S(2)}, u32[]{:S(2)}) collective-permute-start(bf16[128,256]{1,0:T(8,128)(2,1)} %get-tuple-element.40), channel_id=1, source_target_pairs={{0,1},{1,0},{2,3},{3,2},{4,5},{5,4},{6,7},{7,6},{8,9},{9,8},{10,11... | collective-permute-start | bytes 196616 | tf_op jit(solution)/shard_map/ppermute | solution.py:26
  95.1 32.1 %collective-permute-start.3 = (bf16[128,2048]{1,0:T(8,128)(2,1)}, bf16[128,2048]{1,0:T(8,128)(2,1)S(1)}, u32[]{:S(2)}, u32[]{:S(2)}) collective-permute-start(bf16[128,2048]{1,0:T(8,128)(2,1)} %get-tuple-element.38), channel_id=1, source_target_pairs={{0,1},{1,0},{2,3},{3,2},{4,5},{5,4},{6,7},{7,6},{8,9},{9,8},{10,11... | collective-permute-start | bytes 1572872 | tf_op jit(solution)/shard_map/ppermute | solution.py:26
  95.2 6.8 %collective-permute-start.5 = (bf16[128,256]{1,0:T(8,128)(2,1)}, bf16[128,256]{1,0:T(8,128)(2,1)S(1)}, u32[]{:S(2)}, u32[]{:S(2)}) collective-permute-start(bf16[128,256]{1,0:T(8,128)(2,1)} %get-tuple-element.42), channel_id=1, source_target_pairs={{0,1},{1,0},{2,3},{3,2},{4,5},{5,4},{6,7},{7,6},{8,9},{9,8},{10,11... | collective-permute-start | bytes 196616 | tf_op jit(solution)/shard_map/ppermute | solution.py:26
  95.7 18.2 %collective-permute-start.13 = (bf16[80,512]{1,0:T(8,128)(2,1)S(1)}, bf16[80,512]{1,0:T(8,128)(2,1)S(1)}, u32[]{:S(2)}, u32[]{:S(2)}) collective-permute-start(bf16[80,512]{1,0:T(8,128)(2,1)S(1)} %collective-permute-done.7.refs_3_), channel_id=1, source_target_pairs={{0,112},{16,0},{32,16},{48,32},{64,48},{80,64},{96,80},{112,96},{1... | collective-permute-start | bytes 245768 | tf_op jit(solution)/shard_map/ppermute | solution.py:31
  104.7 22.5 %copy-start.2 = (bf16[128,2048]{1,0:T(8,128)(2,1)S(1)}, bf16[128,2048]{1,0:T(8,128)(2,1)}, u32[]{:S(2)}) copy-start(bf16[128,2048]{1,0:T(8,128)(2,1)} %get-tuple-element.37) | copy-start | bytes 1572868
  105.9 14.7 %all-to-all-start.2 = ((bf16[8,16,512]{2,1,0:T(8,128)(2,1)}), bf16[8,16,512]{2,1,0:T(8,128)(2,1)S(1)}, u32[]{:S(2)}, u32[]{:S(2)}) async-start(bf16[8,16,512]{2,1,0:T(8,128)(2,1)} %broadcast_in_dim.19), calls=%async_computation.2 | async-start | bytes 262144 | tf_op jit(solution)/shard_map/all_to_all | solution.py:36
  120.9 7.2 %collective-permute-start.14 = (bf16[8,8,640]{2,1,0:T(8,128)(2,1)S(1)}, bf16[8,8,640]{2,1,0:T(8,128)(2,1)S(1)}, u32[]{:S(2)}, u32[]{:S(2)}) collective-permute-start(bf16[8,8,640]{2,1,0:T(8,128)(2,1)S(1)} %fusion.3), channel_id=1, source_target_pairs={{0,1},{1,0},{2,3},{3,2},{4,5},{5,4},{6,7},{7,6},{8,9},{9,8},{10,11... | collective-permute-start | bytes 245768 | tf_op jit(solution)/shard_map/ppermute | solution.py:26
  128.7 10.6 %all-to-all-start.3 = ((bf16[8,8,640]{2,1,0:T(8,128)(2,1)}), bf16[8,8,640]{2,1,0:T(8,128)(2,1)S(1)}, u32[]{:S(2)}, u32[]{:S(2)}) async-start(bf16[8,8,640]{2,1,0:T(8,128)(2,1)} %fusion), calls=%async_computation.3 | async-start | bytes 163840 | tf_op jit(solution)/shard_map/all_to_all | solution.py:477
